TPU v7x, 32 devices: a whole 2x2x4 slice. The times are simulated.
32 devices in a mesh: spin: 2 (over x), row: 4 (over z), col: 4 (over y, core).
Axes of the slice: x: 2, y: 2, z: 4, core: 2. Of those that a mesh axis runs over, the one named last changes fastest.
Arguments:
- hamiltonian: float32 [5120, 2560], P(('spin', 'row'), 'col'), parts along dimension 0
- bounds: float32 [4], P('spin'), parts along dimension 0
- occ_count: int32 [2], P('spin'), parts along dimension 0
- branches: int32 [12], P('spin'), parts along dimension 0
Outputs:
- output 1: float32 [5120, 2560], P(('spin', 'row'), 'col'), parts along dimension 0
- output 2: float32 [12], P('spin'), parts along dimension 0
- output 3: float32 [2], P('spin'), parts along dimension 0
There are 2 independent parts. A program takes and returns all parts, laid end to end along the dimension named above; each array names one.
All inputs are finite; a program needn't handle non-finite values.
Results may differ from a plain program's by a relative error of at most 0.001.
Values sent between devices are 32-bit elements.
A program may use at most 1 GiB of HBM per device.

v0:
```python
import jax
import jax.numpy as jnp
from jax import lax
from jax.sharding import PartitionSpec as P


def solution(mesh):
    grid_size = mesh.shape["row"]
    left_perm = [(row_pos * grid_size + (row_pos + col_pos) % grid_size, row_pos * grid_size + col_pos) for row_pos in range(grid_size) for col_pos in range(grid_size)]
    right_perm = [(((row_pos + col_pos) % grid_size) * grid_size + col_pos, row_pos * grid_size + col_pos) for row_pos in range(grid_size) for col_pos in range(grid_size)]
    shift_perm = [(src_index, (src_index - 1) % grid_size) for src_index in range(grid_size)]

    def block_product(left_block, right_block):
        return jnp.dot(left_block, right_block, preferred_element_type=jnp.float32, precision=lax.Precision.HIGHEST)

    def grid_square(local_block):
        left_block = lax.ppermute(local_block, ("row", "col"), left_perm)
        right_block = lax.ppermute(local_block, ("row", "col"), right_perm)
        partial_sum = block_product(left_block, right_block)
        for hop_index in range(grid_size - 1):
            left_block = lax.ppermute(left_block, "col", shift_perm)
            right_block = lax.ppermute(right_block, "row", shift_perm)
            partial_sum = partial_sum + block_product(left_block, right_block)
        return partial_sum

    def local_run(ham_block, bounds, occ_count, branches):
        block_size = ham_block.shape[0]
        mat_order = block_size * grid_size
        on_diag = lax.axis_index("row") == lax.axis_index("col")
        diag_mask = jnp.logical_and(jnp.arange(block_size)[:, None] == jnp.arange(block_size)[None, :], on_diag)
        chem_pot = lax.psum(jnp.where(on_diag, jnp.trace(ham_block), 0.0), ("row", "col")) / mat_order
        occupied = occ_count[0].astype(jnp.float32)
        scale_fac = jnp.minimum(occupied / (bounds[1] - chem_pot), (mat_order - occupied) / (chem_pot - bounds[0]))
        density = (scale_fac / mat_order) * (jnp.where(diag_mask, chem_pot, 0.0) - ham_block) + jnp.where(diag_mask, occupied / mat_order, 0.0)
        occ_list = []
        for step_idx in range(branches.shape[0]):
            occ_list.append(lax.psum(jnp.sum(density * density), ("row", "col")))
            squared = grid_square(density)
            density = jnp.where(branches[step_idx] == 1, squared, 2.0 * density - squared)
        energy = lax.psum(2.0 * jnp.sum(density * ham_block), ("row", "col"))
        return density, jnp.stack(occ_list), energy.reshape(1)

    return jax.shard_map(local_run, mesh=mesh, in_specs=(P(("spin", "row"), "col"), P("spin"), P("spin"), P("spin")), out_specs=(P(("spin", "row"), "col"), P("spin"), P("spin")), check_vma=False)
```

profile of v0, /device:TPU:0, one launch (start us, length us, event | category | flops | bytes accessed | tf_op | source)
XLA Modules:
  0.0 1114.1 jit_solution(3244005523025324595)
XLA Ops:
  4.2 35.5 %psum.56 = f32[]{:T(128)} all-reduce(f32[]{:T(128)S(6)} %select_n.61), channel_id=1, replica_groups=mesh['spin'=2,'row'=4,'col'=4] {'row','col'}, use_global_device_ids=true, to_apply=%region_1.2 | all-reduce | flops 1 | bytes 8 | tf_op jit(solution)/shard_map/psum | solution.py:31
  45.0 34.3 %collective-permute-start.2 = (f32[640,640]{1,0:T(8,128)S(1)}, f32[640,640]{1,0:T(8,128)S(1)}, u32[]{:S(2)}, u32[]{:S(2)}) collective-permute-start(f32[640,640]{1,0:T(8,128)S(1)} %collective-permute-done), channel_id=1, source_target_pairs={{0,3},{1,0},{2,1},{3,2},{4,7},{5,4},{6,5},{7,6},{8,11},{9,8},{10,9... | collective-permute-start | bytes 4915208 | tf_op jit(solution)/shard_map/ppermute | solution.py:21
  80.9 24.4 %collective-permute-start.5 = (f32[640,640]{1,0:T(8,128)S(1)}, f32[640,640]{1,0:T(8,128)S(1)}, u32[]{:S(2)}, u32[]{:S(2)}) collective-permute-start(f32[640,640]{1,0:T(8,128)S(1)} %collective-permute-done.3), channel_id=1, source_target_pairs={{0,12},{4,0},{8,4},{12,8},{1,13},{5,1},{9,5},{13,9},{2,14},{6,2},{... | collective-permute-start | bytes 4915208 | tf_op jit(solution)/shard_map/ppermute | solution.py:22
  105.4 28.5 %collective-permute-start.4 = (f32[640,640]{1,0:T(8,128)S(1)}, f32[640,640]{1,0:T(8,128)S(1)}, u32[]{:S(2)}, u32[]{:S(2)}) collective-permute-start(f32[640,640]{1,0:T(8,128)S(1)} %collective-permute-done.2), channel_id=1, source_target_pairs={{0,3},{1,0},{2,1},{3,2},{4,7},{5,4},{6,5},{7,6},{8,11},{9,8},{10,9... | collective-permute-start | bytes 4915208 | tf_op jit(solution)/shard_map/ppermute | solution.py:21
  142.4 10.1 collective-permute-done.4
  152.5 15.6 %collective-permute-start.6 = (f32[640,640]{1,0:T(8,128)S(1)}, f32[640,640]{1,0:T(8,128)S(1)}, u32[]{:S(2)}, u32[]{:S(2)}) collective-permute-start(f32[640,640]{1,0:T(8,128)S(1)} %collective-permute-done.4), channel_id=1, source_target_pairs={{0,3},{1,0},{2,1},{3,2},{4,7},{5,4},{6,5},{7,6},{8,11},{9,8},{10,9... | collective-permute-start | bytes 4915208 | tf_op jit(solution)/shard_map/ppermute | solution.py:21
  178.9 17.8 %fusion.5 = f32[640,640]{1,0:T(8,128)S(1)} fusion(f32[640,640]{1,0:T(8,128)S(1)} %collective-permute-done.4, f32[640,640]{1,0:T(8,128)S(1)} %collective-permute-done.5), kind=kOutput, calls=%fused_computation.21 | convolution fusion | flops 3145728000 | bytes 4915200 | tf_op jit(solution)/shard_map/dot_general | solution.py:14
  196.7 5.7 multiply_reduce_fusion.5
  204.0 8.3 collective-permute-start.11
  212.3 44.2 %collective-permute-start.10 = (f32[640,640]{1,0:T(8,128)S(1)}, f32[640,640]{1,0:T(8,128)S(1)}, u32[]{:S(2)}, u32[]{:S(2)}) collective-permute-start(f32[640,640]{1,0:T(8,128)S(1)} %collective-permute-done.8), channel_id=1, source_target_pairs={{0,3},{1,0},{2,1},{3,2},{4,7},{5,4},{6,5},{7,6},{8,11},{9,8},{10,9... | collective-permute-start | bytes 4915208 | tf_op jit(solution)/shard_map/ppermute | solution.py:21
  256.5 33.7 %collective-permute-start.13 = (f32[640,640]{1,0:T(8,128)S(1)}, f32[640,640]{1,0:T(8,128)S(1)}, u32[]{:S(2)}, u32[]{:S(2)}) collective-permute-start(f32[640,640]{1,0:T(8,128)S(1)} %collective-permute-done.11), channel_id=1, source_target_pairs={{0,12},{4,0},{8,4},{12,8},{1,13},{5,1},{9,5},{13,9},{2,14},{6,2},{... | collective-permute-start | bytes 4915208 | tf_op jit(solution)/shard_map/ppermute | solution.py:22
  290.2 32.4 %collective-permute-start.12 = (f32[640,640]{1,0:T(8,128)S(1)}, f32[640,640]{1,0:T(8,128)S(1)}, u32[]{:S(2)}, u32[]{:S(2)}) collective-permute-start(f32[640,640]{1,0:T(8,128)S(1)} %collective-permute-done.10), channel_id=1, source_target_pairs={{0,3},{1,0},{2,1},{3,2},{4,7},{5,4},{6,5},{7,6},{8,11},{9,8},{10,9... | collective-permute-start | bytes 4915208 | tf_op jit(solution)/shard_map/ppermute | solution.py:21
  325.2 16.1 %collective-permute-done.12 = f32[640,640]{1,0:T(8,128)S(1)} collective-permute-done((f32[640,640]{1,0:T(8,128)S(1)}, f32[640,640]{1,0:T(8,128)S(1)}, u32[]{:S(2)}, u32[]{:S(2)}) %collective-permute-start.12) | collective-permute-done | bytes 1638432 | tf_op jit(solution)/shard_map/ppermute | solution.py:21
  341.3 17.1 %collective-permute-start.14 = (f32[640,640]{1,0:T(8,128)S(1)}, f32[640,640]{1,0:T(8,128)S(1)}, u32[]{:S(2)}, u32[]{:S(2)}) collective-permute-start(f32[640,640]{1,0:T(8,128)S(1)} %collective-permute-done.12), channel_id=1, source_target_pairs={{0,3},{1,0},{2,1},{3,2},{4,7},{5,4},{6,5},{7,6},{8,11},{9,8},{10,9... | collective-permute-start | bytes 4915208 | tf_op jit(solution)/shard_map/ppermute | solution.py:21
  377.0 5.6 multiply_reduce_fusion.4
  384.1 9.0 collective-permute-start.19
  393.2 38.0 %collective-permute-start.18 = (f32[640,640]{1,0:T(8,128)S(1)}, f32[640,640]{1,0:T(8,128)S(1)}, u32[]{:S(2)}, u32[]{:S(2)}) collective-permute-start(f32[640,640]{1,0:T(8,128)S(1)} %collective-permute-done.16), channel_id=1, source_target_pairs={{0,3},{1,0},{2,1},{3,2},{4,7},{5,4},{6,5},{7,6},{8,11},{9,8},{10,9... | collective-permute-start | bytes 4915208 | tf_op jit(solution)/shard_map/ppermute | solution.py:21
  431.2 35.7 %collective-permute-start.21 = (f32[640,640]{1,0:T(8,128)S(1)}, f32[640,640]{1,0:T(8,128)S(1)}, u32[]{:S(2)}, u32[]{:S(2)}) collective-permute-start(f32[640,640]{1,0:T(8,128)S(1)} %collective-permute-done.19), channel_id=1, source_target_pairs={{0,12},{4,0},{8,4},{12,8},{1,13},{5,1},{9,5},{13,9},{2,14},{6,2},{... | collective-permute-start | bytes 4915208 | tf_op jit(solution)/shard_map/ppermute | solution.py:22
  466.9 27.7 %collective-permute-start.20 = (f32[640,640]{1,0:T(8,128)S(1)}, f32[640,640]{1,0:T(8,128)S(1)}, u32[]{:S(2)}, u32[]{:S(2)}) collective-permute-start(f32[640,640]{1,0:T(8,128)S(1)} %collective-permute-done.18), channel_id=1, source_target_pairs={{0,3},{1,0},{2,1},{3,2},{4,7},{5,4},{6,5},{7,6},{8,11},{9,8},{10,9... | collective-permute-start | bytes 4915208 | tf_op jit(solution)/shard_map/ppermute | solution.py:21
  497.1 16.1 %collective-permute-done.20 = f32[640,640]{1,0:T(8,128)S(1)} collective-permute-done((f32[640,640]{1,0:T(8,128)S(1)}, f32[640,640]{1,0:T(8,128)S(1)}, u32[]{:S(2)}, u32[]{:S(2)}) %collective-permute-start.20) | collective-permute-done | bytes 1638432 | tf_op jit(solution)/shard_map/ppermute | solution.py:21
  513.2 15.8 %collective-permute-start.22 = (f32[640,640]{1,0:T(8,128)S(1)}, f32[640,640]{1,0:T(8,128)S(1)}, u32[]{:S(2)}, u32[]{:S(2)}) collective-permute-start(f32[640,640]{1,0:T(8,128)S(1)} %collective-permute-done.20), channel_id=1, source_target_pairs={{0,3},{1,0},{2,1},{3,2},{4,7},{5,4},{6,5},{7,6},{8,11},{9,8},{10,9... | collective-permute-start | bytes 4915208 | tf_op jit(solution)/shard_map/ppermute | solution.py:21
  547.6 5.7 multiply_reduce_fusion.3
  554.8 20.0 %collective-permute-start.27 = (f32[640,640]{1,0:T(8,128)S(1)}, f32[640,640]{1,0:T(8,128)S(1)}, u32[]{:S(2)}, u32[]{:S(2)}) collective-permute-start(f32[640,640]{1,0:T(8,128)S(1)} %collective-permute-done.25), channel_id=1, source_target_pairs={{0,12},{4,0},{8,4},{12,8},{1,13},{5,1},{9,5},{13,9},{2,14},{6,2},{... | collective-permute-start | bytes 4915208 | tf_op jit(solution)/shard_map/ppermute | solution.py:22
  574.9 22.4 %collective-permute-start.26 = (f32[640,640]{1,0:T(8,128)S(1)}, f32[640,640]{1,0:T(8,128)S(1)}, u32[]{:S(2)}, u32[]{:S(2)}) collective-permute-start(f32[640,640]{1,0:T(8,128)S(1)} %collective-permute-done.24), channel_id=1, source_target_pairs={{0,3},{1,0},{2,1},{3,2},{4,7},{5,4},{6,5},{7,6},{8,11},{9,8},{10,9... | collective-permute-start | bytes 4915208 | tf_op jit(solution)/shard_map/ppermute | solution.py:21
  597.2 11.3 %collective-permute-done.27 = f32[640,640]{1,0:T(8,128)S(1)} collective-permute-done((f32[640,640]{1,0:T(8,128)S(1)}, f32[640,640]{1,0:T(8,128)S(1)}, u32[]{:S(2)}, u32[]{:S(2)}) %collective-permute-start.27) | collective-permute-done | bytes 1638432 | tf_op jit(solution)/shard_map/ppermute | solution.py:22
  608.5 27.9 %collective-permute-start.29 = (f32[640,640]{1,0:T(8,128)S(1)}, f32[640,640]{1,0:T(8,128)S(1)}, u32[]{:S(2)}, u32[]{:S(2)}) collective-permute-start(f32[640,640]{1,0:T(8,128)S(1)} %collective-permute-done.27), channel_id=1, source_target_pairs={{0,12},{4,0},{8,4},{12,8},{1,13},{5,1},{9,5},{13,9},{2,14},{6,2},{... | collective-permute-start | bytes 4915208 | tf_op jit(solution)/shard_map/ppermute | solution.py:22
  636.4 25.3 %collective-permute-start.28 = (f32[640,640]{1,0:T(8,128)S(1)}, f32[640,640]{1,0:T(8,128)S(1)}, u32[]{:S(2)}, u32[]{:S(2)}) collective-permute-start(f32[640,640]{1,0:T(8,128)S(1)} %collective-permute-done.26), channel_id=1, source_target_pairs={{0,3},{1,0},{2,1},{3,2},{4,7},{5,4},{6,5},{7,6},{8,11},{9,8},{10,9... | collective-permute-start | bytes 4915208 | tf_op jit(solution)/shard_map/ppermute | solution.py:21
  661.7 6.8 collective-permute-done.29
  672.8 7.5 collective-permute-done.28
  680.3 15.6 %collective-permute-start.30 = (f32[640,640]{1,0:T(8,128)S(1)}, f32[640,640]{1,0:T(8,128)S(1)}, u32[]{:S(2)}, u32[]{:S(2)}) collective-permute-start(f32[640,640]{1,0:T(8,128)S(1)} %collective-permute-done.28), channel_id=1, source_target_pairs={{0,3},{1,0},{2,1},{3,2},{4,7},{5,4},{6,5},{7,6},{8,11},{9,8},{10,9... | collective-permute-start | bytes 4915208 | tf_op jit(solution)/shard_map/ppermute | solution.py:21
  714.6 5.6 multiply_reduce_fusion.2
  721.7 24.8 %collective-permute-start.35 = (f32[640,640]{1,0:T(8,128)S(1)}, f32[640,640]{1,0:T(8,128)S(1)}, u32[]{:S(2)}, u32[]{:S(2)}) collective-permute-start(f32[640,640]{1,0:T(8,128)S(1)} %collective-permute-done.33), channel_id=1, source_target_pairs={{0,12},{4,0},{8,4},{12,8},{1,13},{5,1},{9,5},{13,9},{2,14},{6,2},{... | collective-permute-start | bytes 4915208 | tf_op jit(solution)/shard_map/ppermute | solution.py:22
  746.5 20.3 %collective-permute-start.34 = (f32[640,640]{1,0:T(8,128)S(1)}, f32[640,640]{1,0:T(8,128)S(1)}, u32[]{:S(2)}, u32[]{:S(2)}) collective-permute-start(f32[640,640]{1,0:T(8,128)S(1)} %collective-permute-done.32), channel_id=1, source_target_pairs={{0,3},{1,0},{2,1},{3,2},{4,7},{5,4},{6,5},{7,6},{8,11},{9,8},{10,9... | collective-permute-start | bytes 4915208 | tf_op jit(solution)/shard_map/ppermute | solution.py:21
  766.8 13.4 %collective-permute-done.35 = f32[640,640]{1,0:T(8,128)S(1)} collective-permute-done((f32[640,640]{1,0:T(8,128)S(1)}, f32[640,640]{1,0:T(8,128)S(1)}, u32[]{:S(2)}, u32[]{:S(2)}) %collective-permute-start.35) | collective-permute-done | bytes 1638432 | tf_op jit(solution)/shard_map/ppermute | solution.py:22
  780.2 21.3 %collective-permute-start.37 = (f32[640,640]{1,0:T(8,128)S(1)}, f32[640,640]{1,0:T(8,128)S(1)}, u32[]{:S(2)}, u32[]{:S(2)}) collective-permute-start(f32[640,640]{1,0:T(8,128)S(1)} %collective-permute-done.35), channel_id=1, source_target_pairs={{0,12},{4,0},{8,4},{12,8},{1,13},{5,1},{9,5},{13,9},{2,14},{6,2},{... | collective-permute-start | bytes 4915208 | tf_op jit(solution)/shard_map/ppermute | solution.py:22
  801.4 23.0 %collective-permute-start.36 = (f32[640,640]{1,0:T(8,128)S(1)}, f32[640,640]{1,0:T(8,128)S(1)}, u32[]{:S(2)}, u32[]{:S(2)}) collective-permute-start(f32[640,640]{1,0:T(8,128)S(1)} %collective-permute-done.34), channel_id=1, source_target_pairs={{0,3},{1,0},{2,1},{3,2},{4,7},{5,4},{6,5},{7,6},{8,11},{9,8},{10,9... | collective-permute-start | bytes 4915208 | tf_op jit(solution)/shard_map/ppermute | solution.py:21
  824.4 12.7 %collective-permute-done.37 = f32[640,640]{1,0:T(8,128)S(1)} collective-permute-done((f32[640,640]{1,0:T(8,128)S(1)}, f32[640,640]{1,0:T(8,128)S(1)}, u32[]{:S(2)}, u32[]{:S(2)}) %collective-permute-start.37) | collective-permute-done | bytes 1638432 | tf_op jit(solution)/shard_map/ppermute | solution.py:22
  843.0 16.0 %collective-permute-start.38 = (f32[640,640]{1,0:T(8,128)S(1)}, f32[640,640]{1,0:T(8,128)S(1)}, u32[]{:S(2)}, u32[]{:S(2)}) collective-permute-start(f32[640,640]{1,0:T(8,128)S(1)} %collective-permute-done.36), channel_id=1, source_target_pairs={{0,3},{1,0},{2,1},{3,2},{4,7},{5,4},{6,5},{7,6},{8,11},{9,8},{10,9... | collective-permute-start | bytes 4915208 | tf_op jit(solution)/shard_map/ppermute | solution.py:21
  877.7 5.6 multiply_reduce_fusion.1
  884.8 29.4 %collective-permute-start.43 = (f32[640,640]{1,0:T(8,128)S(1)}, f32[640,640]{1,0:T(8,128)S(1)}, u32[]{:S(2)}, u32[]{:S(2)}) collective-permute-start(f32[640,640]{1,0:T(8,128)S(1)} %collective-permute-done.41), channel_id=1, source_target_pairs={{0,12},{4,0},{8,4},{12,8},{1,13},{5,1},{9,5},{13,9},{2,14},{6,2},{... | collective-permute-start | bytes 4915208 | tf_op jit(solution)/shard_map/ppermute | solution.py:22
  914.2 22.8 %collective-permute-start.42 = (f32[640,640]{1,0:T(8,128)S(1)}, f32[640,640]{1,0:T(8,128)S(1)}, u32[]{:S(2)}, u32[]{:S(2)}) collective-permute-start(f32[640,640]{1,0:T(8,128)S(1)} %collective-permute-done.40), channel_id=1, source_target_pairs={{0,3},{1,0},{2,1},{3,2},{4,7},{5,4},{6,5},{7,6},{8,11},{9,8},{10,9... | collective-permute-start | bytes 4915208 | tf_op jit(solution)/shard_map/ppermute | solution.py:21
  936.9 10.9 collective-permute-done.43
  947.8 22.8 %collective-permute-start.45 = (f32[640,640]{1,0:T(8,128)S(1)}, f32[640,640]{1,0:T(8,128)S(1)}, u32[]{:S(2)}, u32[]{:S(2)}) collective-permute-start(f32[640,640]{1,0:T(8,128)S(1)} %collective-permute-done.43), channel_id=1, source_target_pairs={{0,12},{4,0},{8,4},{12,8},{1,13},{5,1},{9,5},{13,9},{2,14},{6,2},{... | collective-permute-start | bytes 4915208 | tf_op jit(solution)/shard_map/ppermute | solution.py:22
  970.6 24.4 %collective-permute-start.44 = (f32[640,640]{1,0:T(8,128)S(1)}, f32[640,640]{1,0:T(8,128)S(1)}, u32[]{:S(2)}, u32[]{:S(2)}) collective-permute-start(f32[640,640]{1,0:T(8,128)S(1)} %collective-permute-done.42), channel_id=1, source_target_pairs={{0,3},{1,0},{2,1},{3,2},{4,7},{5,4},{6,5},{7,6},{8,11},{9,8},{10,9... | collective-permute-start | bytes 4915208 | tf_op jit(solution)/shard_map/ppermute | solution.py:21
  995.0 11.2 %collective-permute-done.45 = f32[640,640]{1,0:T(8,128)S(1)} collective-permute-done((f32[640,640]{1,0:T(8,128)S(1)}, f32[640,640]{1,0:T(8,128)S(1)}, u32[]{:S(2)}, u32[]{:S(2)}) %collective-permute-start.45) | collective-permute-done | bytes 1638432 | tf_op jit(solution)/shard_map/ppermute | solution.py:22
  1013.7 15.6 %collective-permute-start.46 = (f32[640,640]{1,0:T(8,128)S(1)}, f32[640,640]{1,0:T(8,128)S(1)}, u32[]{:S(2)}, u32[]{:S(2)}) collective-permute-start(f32[640,640]{1,0:T(8,128)S(1)} %collective-permute-done.44), channel_id=1, source_target_pairs={{0,3},{1,0},{2,1},{3,2},{4,7},{5,4},{6,5},{7,6},{8,11},{9,8},{10,9... | collective-permute-start | bytes 4915208 | tf_op jit(solution)/shard_map/ppermute | solution.py:21
  1047.9 6.5 multiply_reduce_fusion
  1055.1 54.3 %all-reduce = (f32[1]{0:T(128)}, f32[1]{0:T(128)}, f32[1]{0:T(128)}, f32[1]{0:T(128)}, f32[1]{0:T(128)}, /*index=5*/f32[1]{0:T(128)}, f32[1]{0:T(128)}) all-reduce(f32[1]{0:T(128)} %bitcast.9, f32[1]{0:T(128)} %bitcast.10, f32[1]{0:T(128)} %bitcast.11, f32[1]{0:T(128)} %bitcast.12, ...), channel_id=1, replica_groups=mesh['spin'=2,'row'=4,'col'=4] {'row','col'}, use_global_device_ids=true, to_apply=%region_3.4 | all-reduce | flops 7 | bytes 56 | tf_op jit(solution)/shard_map/psum | solution.py:37
  (85 shorter events, 150.2 us)
Async XLA Ops:
  43.4 1.5 collective-permute-start.1
  44.1 0.9 collective-permute-start
  44.9 36.0 %collective-permute-start.3 = (f32[640,640]{1,0:T(8,128)S(1)}, f32[640,640]{1,0:T(8,128)S(1)}, u32[]{:S(2)}, u32[]{:S(2)}) collective-permute-start(f32[640,640]{1,0:T(8,128)S(1)} %collective-permute-done.1), channel_id=1, source_target_pairs={{0,12},{4,0},{8,4},{12,8},{1,13},{5,1},{9,5},{13,9},{2,14},{6,2},{... | collective-permute-start | bytes 4915208 | tf_op jit(solution)/shard_map/ppermute | solution.py:22
  45.0 60.3 %collective-permute-start.2 = (f32[640,640]{1,0:T(8,128)S(1)}, f32[640,640]{1,0:T(8,128)S(1)}, u32[]{:S(2)}, u32[]{:S(2)}) collective-permute-start(f32[640,640]{1,0:T(8,128)S(1)} %collective-permute-done), channel_id=1, source_target_pairs={{0,3},{1,0},{2,1},{3,2},{4,7},{5,4},{6,5},{7,6},{8,11},{9,8},{10,9... | collective-permute-start | bytes 4915208 | tf_op jit(solution)/shard_map/ppermute | solution.py:21
  80.9 57.2 %collective-permute-start.5 = (f32[640,640]{1,0:T(8,128)S(1)}, f32[640,640]{1,0:T(8,128)S(1)}, u32[]{:S(2)}, u32[]{:S(2)}) collective-permute-start(f32[640,640]{1,0:T(8,128)S(1)} %collective-permute-done.3), channel_id=1, source_target_pairs={{0,12},{4,0},{8,4},{12,8},{1,13},{5,1},{9,5},{13,9},{2,14},{6,2},{... | collective-permute-start | bytes 4915208 | tf_op jit(solution)/shard_map/ppermute | solution.py:22
  105.4 47.1 %collective-permute-start.4 = (f32[640,640]{1,0:T(8,128)S(1)}, f32[640,640]{1,0:T(8,128)S(1)}, u32[]{:S(2)}, u32[]{:S(2)}) collective-permute-start(f32[640,640]{1,0:T(8,128)S(1)} %collective-permute-done.2), channel_id=1, source_target_pairs={{0,3},{1,0},{2,1},{3,2},{4,7},{5,4},{6,5},{7,6},{8,11},{9,8},{10,9... | collective-permute-start | bytes 4915208 | tf_op jit(solution)/shard_map/ppermute | solution.py:21
  138.1 58.6 %collective-permute-start.7 = (f32[640,640]{1,0:T(8,128)S(1)}, f32[640,640]{1,0:T(8,128)S(1)}, u32[]{:S(2)}, u32[]{:S(2)}) collective-permute-start(f32[640,640]{1,0:T(8,128)S(1)} %collective-permute-done.5), channel_id=1, source_target_pairs={{0,12},{4,0},{8,4},{12,8},{1,13},{5,1},{9,5},{13,9},{2,14},{6,2},{... | collective-permute-start | bytes 4915208 | tf_op jit(solution)/shard_map/ppermute | solution.py:22
  152.5 44.2 %collective-permute-start.6 = (f32[640,640]{1,0:T(8,128)S(1)}, f32[640,640]{1,0:T(8,128)S(1)}, u32[]{:S(2)}, u32[]{:S(2)}) collective-permute-start(f32[640,640]{1,0:T(8,128)S(1)} %collective-permute-done.4), channel_id=1, source_target_pairs={{0,3},{1,0},{2,1},{3,2},{4,7},{5,4},{6,5},{7,6},{8,11},{9,8},{10,9... | collective-permute-start | bytes 4915208 | tf_op jit(solution)/shard_map/ppermute | solution.py:21
  202.4 1.5 collective-permute-start.9
  203.2 9.1 collective-permute-start.8
  204.0 52.6 %collective-permute-start.11 = (f32[640,640]{1,0:T(8,128)S(1)}, f32[640,640]{1,0:T(8,128)S(1)}, u32[]{:S(2)}, u32[]{:S(2)}) collective-permute-start(f32[640,640]{1,0:T(8,128)S(1)} %collective-permute-done.9), channel_id=1, source_target_pairs={{0,12},{4,0},{8,4},{12,8},{1,13},{5,1},{9,5},{13,9},{2,14},{6,2},{... | collective-permute-start | bytes 4915208 | tf_op jit(solution)/shard_map/ppermute | solution.py:22
  212.3 78.0 %collective-permute-start.10 = (f32[640,640]{1,0:T(8,128)S(1)}, f32[640,640]{1,0:T(8,128)S(1)}, u32[]{:S(2)}, u32[]{:S(2)}) collective-permute-start(f32[640,640]{1,0:T(8,128)S(1)} %collective-permute-done.8), channel_id=1, source_target_pairs={{0,3},{1,0},{2,1},{3,2},{4,7},{5,4},{6,5},{7,6},{8,11},{9,8},{10,9... | collective-permute-start | bytes 4915208 | tf_op jit(solution)/shard_map/ppermute | solution.py:21
  256.5 66.1 %collective-permute-start.13 = (f32[640,640]{1,0:T(8,128)S(1)}, f32[640,640]{1,0:T(8,128)S(1)}, u32[]{:S(2)}, u32[]{:S(2)}) collective-permute-start(f32[640,640]{1,0:T(8,128)S(1)} %collective-permute-done.11), channel_id=1, source_target_pairs={{0,12},{4,0},{8,4},{12,8},{1,13},{5,1},{9,5},{13,9},{2,14},{6,2},{... | collective-permute-start | bytes 4915208 | tf_op jit(solution)/shard_map/ppermute | solution.py:22
  290.2 51.0 %collective-permute-start.12 = (f32[640,640]{1,0:T(8,128)S(1)}, f32[640,640]{1,0:T(8,128)S(1)}, u32[]{:S(2)}, u32[]{:S(2)}) collective-permute-start(f32[640,640]{1,0:T(8,128)S(1)} %collective-permute-done.10), channel_id=1, source_target_pairs={{0,3},{1,0},{2,1},{3,2},{4,7},{5,4},{6,5},{7,6},{8,11},{9,8},{10,9... | collective-permute-start | bytes 4915208 | tf_op jit(solution)/shard_map/ppermute | solution.py:21
  322.7 50.8 %collective-permute-start.15 = (f32[640,640]{1,0:T(8,128)S(1)}, f32[640,640]{1,0:T(8,128)S(1)}, u32[]{:S(2)}, u32[]{:S(2)}) collective-permute-start(f32[640,640]{1,0:T(8,128)S(1)} %collective-permute-done.13), channel_id=1, source_target_pairs={{0,12},{4,0},{8,4},{12,8},{1,13},{5,1},{9,5},{13,9},{2,14},{6,2},{... | collective-permute-start | bytes 4915208 | tf_op jit(solution)/shard_map/ppermute | solution.py:22
  341.3 35.7 %collective-permute-start.14 = (f32[640,640]{1,0:T(8,128)S(1)}, f32[640,640]{1,0:T(8,128)S(1)}, u32[]{:S(2)}, u32[]{:S(2)}) collective-permute-start(f32[640,640]{1,0:T(8,128)S(1)} %collective-permute-done.12), channel_id=1, source_target_pairs={{0,3},{1,0},{2,1},{3,2},{4,7},{5,4},{6,5},{7,6},{8,11},{9,8},{10,9... | collective-permute-start | bytes 4915208 | tf_op jit(solution)/shard_map/ppermute | solution.py:21
  382.6 1.5 collective-permute-start.17
  383.4 9.8 collective-permute-start.16
  384.1 47.0 %collective-permute-start.19 = (f32[640,640]{1,0:T(8,128)S(1)}, f32[640,640]{1,0:T(8,128)S(1)}, u32[]{:S(2)}, u32[]{:S(2)}) collective-permute-start(f32[640,640]{1,0:T(8,128)S(1)} %collective-permute-done.17), channel_id=1, source_target_pairs={{0,12},{4,0},{8,4},{12,8},{1,13},{5,1},{9,5},{13,9},{2,14},{6,2},{... | collective-permute-start | bytes 4915208 | tf_op jit(solution)/shard_map/ppermute | solution.py:22
  393.2 73.8 %collective-permute-start.18 = (f32[640,640]{1,0:T(8,128)S(1)}, f32[640,640]{1,0:T(8,128)S(1)}, u32[]{:S(2)}, u32[]{:S(2)}) collective-permute-start(f32[640,640]{1,0:T(8,128)S(1)} %collective-permute-done.16), channel_id=1, source_target_pairs={{0,3},{1,0},{2,1},{3,2},{4,7},{5,4},{6,5},{7,6},{8,11},{9,8},{10,9... | collective-permute-start | bytes 4915208 | tf_op jit(solution)/shard_map/ppermute | solution.py:21
  431.2 63.4 %collective-permute-start.21 = (f32[640,640]{1,0:T(8,128)S(1)}, f32[640,640]{1,0:T(8,128)S(1)}, u32[]{:S(2)}, u32[]{:S(2)}) collective-permute-start(f32[640,640]{1,0:T(8,128)S(1)} %collective-permute-done.19), channel_id=1, source_target_pairs={{0,12},{4,0},{8,4},{12,8},{1,13},{5,1},{9,5},{13,9},{2,14},{6,2},{... | collective-permute-start | bytes 4915208 | tf_op jit(solution)/shard_map/ppermute | solution.py:22
  466.9 46.3 %collective-permute-start.20 = (f32[640,640]{1,0:T(8,128)S(1)}, f32[640,640]{1,0:T(8,128)S(1)}, u32[]{:S(2)}, u32[]{:S(2)}) collective-permute-start(f32[640,640]{1,0:T(8,128)S(1)} %collective-permute-done.18), channel_id=1, source_target_pairs={{0,3},{1,0},{2,1},{3,2},{4,7},{5,4},{6,5},{7,6},{8,11},{9,8},{10,9... | collective-permute-start | bytes 4915208 | tf_op jit(solution)/shard_map/ppermute | solution.py:21
  494.6 49.6 %collective-permute-start.23 = (f32[640,640]{1,0:T(8,128)S(1)}, f32[640,640]{1,0:T(8,128)S(1)}, u32[]{:S(2)}, u32[]{:S(2)}) collective-permute-start(f32[640,640]{1,0:T(8,128)S(1)} %collective-permute-done.21), channel_id=1, source_target_pairs={{0,12},{4,0},{8,4},{12,8},{1,13},{5,1},{9,5},{13,9},{2,14},{6,2},{... | collective-permute-start | bytes 4915208 | tf_op jit(solution)/shard_map/ppermute | solution.py:22
  513.2 34.4 %collective-permute-start.22 = (f32[640,640]{1,0:T(8,128)S(1)}, f32[640,640]{1,0:T(8,128)S(1)}, u32[]{:S(2)}, u32[]{:S(2)}) collective-permute-start(f32[640,640]{1,0:T(8,128)S(1)} %collective-permute-done.20), channel_id=1, source_target_pairs={{0,3},{1,0},{2,1},{3,2},{4,7},{5,4},{6,5},{7,6},{8,11},{9,8},{10,9... | collective-permute-start | bytes 4915208 | tf_op jit(solution)/shard_map/ppermute | solution.py:21
  553.3 1.5 collective-permute-start.25
  554.0 20.8 %collective-permute-start.24 = (f32[640,640]{1,0:T(8,128)S(1)}, f32[640,640]{1,0:T(8,128)S(1)}, u32[]{:S(2)}, u32[]{:S(2)}) collective-permute-start(f32[640,640]{1,0:T(8,128)S(1)} %get-tuple-element.25), channel_id=1, source_target_pairs={{0,0},{1,1},{2,2},{3,3},{5,4},{6,5},{7,6},{4,7},{10,8},{11,9},{8,1... | collective-permute-start | bytes 4915208 | tf_op jit(solution)/shard_map/ppermute | solution.py:17
  554.8 53.7 %collective-permute-start.27 = (f32[640,640]{1,0:T(8,128)S(1)}, f32[640,640]{1,0:T(8,128)S(1)}, u32[]{:S(2)}, u32[]{:S(2)}) collective-permute-start(f32[640,640]{1,0:T(8,128)S(1)} %collective-permute-done.25), channel_id=1, source_target_pairs={{0,12},{4,0},{8,4},{12,8},{1,13},{5,1},{9,5},{13,9},{2,14},{6,2},{... | collective-permute-start | bytes 4915208 | tf_op jit(solution)/shard_map/ppermute | solution.py:22
  574.9 61.6 %collective-permute-start.26 = (f32[640,640]{1,0:T(8,128)S(1)}, f32[640,640]{1,0:T(8,128)S(1)}, u32[]{:S(2)}, u32[]{:S(2)}) collective-permute-start(f32[640,640]{1,0:T(8,128)S(1)} %collective-permute-done.24), channel_id=1, source_target_pairs={{0,3},{1,0},{2,1},{3,2},{4,7},{5,4},{6,5},{7,6},{8,11},{9,8},{10,9... | collective-permute-start | bytes 4915208 | tf_op jit(solution)/shard_map/ppermute | solution.py:21
  608.5 60.0 %collective-permute-start.29 = (f32[640,640]{1,0:T(8,128)S(1)}, f32[640,640]{1,0:T(8,128)S(1)}, u32[]{:S(2)}, u32[]{:S(2)}) collective-permute-start(f32[640,640]{1,0:T(8,128)S(1)} %collective-permute-done.27), channel_id=1, source_target_pairs={{0,12},{4,0},{8,4},{12,8},{1,13},{5,1},{9,5},{13,9},{2,14},{6,2},{... | collective-permute-start | bytes 4915208 | tf_op jit(solution)/shard_map/ppermute | solution.py:22
  636.4 43.9 %collective-permute-start.28 = (f32[640,640]{1,0:T(8,128)S(1)}, f32[640,640]{1,0:T(8,128)S(1)}, u32[]{:S(2)}, u32[]{:S(2)}) collective-permute-start(f32[640,640]{1,0:T(8,128)S(1)} %collective-permute-done.26), channel_id=1, source_target_pairs={{0,3},{1,0},{2,1},{3,2},{4,7},{5,4},{6,5},{7,6},{8,11},{9,8},{10,9... | collective-permute-start | bytes 4915208 | tf_op jit(solution)/shard_map/ppermute | solution.py:21
  668.5 42.3 %collective-permute-start.31 = (f32[640,640]{1,0:T(8,128)S(1)}, f32[640,640]{1,0:T(8,128)S(1)}, u32[]{:S(2)}, u32[]{:S(2)}) collective-permute-start(f32[640,640]{1,0:T(8,128)S(1)} %collective-permute-done.29), channel_id=1, source_target_pairs={{0,12},{4,0},{8,4},{12,8},{1,13},{5,1},{9,5},{13,9},{2,14},{6,2},{... | collective-permute-start | bytes 4915208 | tf_op jit(solution)/shard_map/ppermute | solution.py:22
  680.3 34.3 %collective-permute-start.30 = (f32[640,640]{1,0:T(8,128)S(1)}, f32[640,640]{1,0:T(8,128)S(1)}, u32[]{:S(2)}, u32[]{:S(2)}) collective-permute-start(f32[640,640]{1,0:T(8,128)S(1)} %collective-permute-done.28), channel_id=1, source_target_pairs={{0,3},{1,0},{2,1},{3,2},{4,7},{5,4},{6,5},{7,6},{8,11},{9,8},{10,9... | collective-permute-start | bytes 4915208 | tf_op jit(solution)/shard_map/ppermute | solution.py:21
  720.2 1.5 collective-permute-start.33
  721.0 25.6 %collective-permute-start.32 = (f32[640,640]{1,0:T(8,128)S(1)}, f32[640,640]{1,0:T(8,128)S(1)}, u32[]{:S(2)}, u32[]{:S(2)}) collective-permute-start(f32[640,640]{1,0:T(8,128)S(1)} %get-tuple-element.27), channel_id=1, source_target_pairs={{0,0},{1,1},{2,2},{3,3},{5,4},{6,5},{7,6},{4,7},{10,8},{11,9},{8,1... | collective-permute-start | bytes 4915208 | tf_op jit(solution)/shard_map/ppermute | solution.py:17
  721.7 58.4 %collective-permute-start.35 = (f32[640,640]{1,0:T(8,128)S(1)}, f32[640,640]{1,0:T(8,128)S(1)}, u32[]{:S(2)}, u32[]{:S(2)}) collective-permute-start(f32[640,640]{1,0:T(8,128)S(1)} %collective-permute-done.33), channel_id=1, source_target_pairs={{0,12},{4,0},{8,4},{12,8},{1,13},{5,1},{9,5},{13,9},{2,14},{6,2},{... | collective-permute-start | bytes 4915208 | tf_op jit(solution)/shard_map/ppermute | solution.py:22
  746.5 54.9 %collective-permute-start.34 = (f32[640,640]{1,0:T(8,128)S(1)}, f32[640,640]{1,0:T(8,128)S(1)}, u32[]{:S(2)}, u32[]{:S(2)}) collective-permute-start(f32[640,640]{1,0:T(8,128)S(1)} %collective-permute-done.32), channel_id=1, source_target_pairs={{0,3},{1,0},{2,1},{3,2},{4,7},{5,4},{6,5},{7,6},{8,11},{9,8},{10,9... | collective-permute-start | bytes 4915208 | tf_op jit(solution)/shard_map/ppermute | solution.py:21
  780.2 56.9 %collective-permute-start.37 = (f32[640,640]{1,0:T(8,128)S(1)}, f32[640,640]{1,0:T(8,128)S(1)}, u32[]{:S(2)}, u32[]{:S(2)}) collective-permute-start(f32[640,640]{1,0:T(8,128)S(1)} %collective-permute-done.35), channel_id=1, source_target_pairs={{0,12},{4,0},{8,4},{12,8},{1,13},{5,1},{9,5},{13,9},{2,14},{6,2},{... | collective-permute-start | bytes 4915208 | tf_op jit(solution)/shard_map/ppermute | solution.py:22
  801.4 41.6 %collective-permute-start.36 = (f32[640,640]{1,0:T(8,128)S(1)}, f32[640,640]{1,0:T(8,128)S(1)}, u32[]{:S(2)}, u32[]{:S(2)}) collective-permute-start(f32[640,640]{1,0:T(8,128)S(1)} %collective-permute-done.34), channel_id=1, source_target_pairs={{0,3},{1,0},{2,1},{3,2},{4,7},{5,4},{6,5},{7,6},{8,11},{9,8},{10,9... | collective-permute-start | bytes 4915208 | tf_op jit(solution)/shard_map/ppermute | solution.py:21
  837.1 40.5 %collective-permute-start.39 = (f32[640,640]{1,0:T(8,128)S(1)}, f32[640,640]{1,0:T(8,128)S(1)}, u32[]{:S(2)}, u32[]{:S(2)}) collective-permute-start(f32[640,640]{1,0:T(8,128)S(1)} %collective-permute-done.37), channel_id=1, source_target_pairs={{0,12},{4,0},{8,4},{12,8},{1,13},{5,1},{9,5},{13,9},{2,14},{6,2},{... | collective-permute-start | bytes 4915208 | tf_op jit(solution)/shard_map/ppermute | solution.py:22
  843.0 34.6 %collective-permute-start.38 = (f32[640,640]{1,0:T(8,128)S(1)}, f32[640,640]{1,0:T(8,128)S(1)}, u32[]{:S(2)}, u32[]{:S(2)}) collective-permute-start(f32[640,640]{1,0:T(8,128)S(1)} %collective-permute-done.36), channel_id=1, source_target_pairs={{0,3},{1,0},{2,1},{3,2},{4,7},{5,4},{6,5},{7,6},{8,11},{9,8},{10,9... | collective-permute-start | bytes 4915208 | tf_op jit(solution)/shard_map/ppermute | solution.py:21
  883.2 1.5 collective-permute-start.41
  884.0 30.2 %collective-permute-start.40 = (f32[640,640]{1,0:T(8,128)S(1)}, f32[640,640]{1,0:T(8,128)S(1)}, u32[]{:S(2)}, u32[]{:S(2)}) collective-permute-start(f32[640,640]{1,0:T(8,128)S(1)} %get-tuple-element.29), channel_id=1, source_target_pairs={{0,0},{1,1},{2,2},{3,3},{5,4},{6,5},{7,6},{4,7},{10,8},{11,9},{8,1... | collective-permute-start | bytes 4915208 | tf_op jit(solution)/shard_map/ppermute | solution.py:17
  884.8 63.0 %collective-permute-start.43 = (f32[640,640]{1,0:T(8,128)S(1)}, f32[640,640]{1,0:T(8,128)S(1)}, u32[]{:S(2)}, u32[]{:S(2)}) collective-permute-start(f32[640,640]{1,0:T(8,128)S(1)} %collective-permute-done.41), channel_id=1, source_target_pairs={{0,12},{4,0},{8,4},{12,8},{1,13},{5,1},{9,5},{13,9},{2,14},{6,2},{... | collective-permute-start | bytes 4915208 | tf_op jit(solution)/shard_map/ppermute | solution.py:22
  914.2 56.5 %collective-permute-start.42 = (f32[640,640]{1,0:T(8,128)S(1)}, f32[640,640]{1,0:T(8,128)S(1)}, u32[]{:S(2)}, u32[]{:S(2)}) collective-permute-start(f32[640,640]{1,0:T(8,128)S(1)} %collective-permute-done.40), channel_id=1, source_target_pairs={{0,3},{1,0},{2,1},{3,2},{4,7},{5,4},{6,5},{7,6},{8,11},{9,8},{10,9... | collective-permute-start | bytes 4915208 | tf_op jit(solution)/shard_map/ppermute | solution.py:21
  947.8 58.4 %collective-permute-start.45 = (f32[640,640]{1,0:T(8,128)S(1)}, f32[640,640]{1,0:T(8,128)S(1)}, u32[]{:S(2)}, u32[]{:S(2)}) collective-permute-start(f32[640,640]{1,0:T(8,128)S(1)} %collective-permute-done.43), channel_id=1, source_target_pairs={{0,12},{4,0},{8,4},{12,8},{1,13},{5,1},{9,5},{13,9},{2,14},{6,2},{... | collective-permute-start | bytes 4915208 | tf_op jit(solution)/shard_map/ppermute | solution.py:22
  970.6 43.0 %collective-permute-start.44 = (f32[640,640]{1,0:T(8,128)S(1)}, f32[640,640]{1,0:T(8,128)S(1)}, u32[]{:S(2)}, u32[]{:S(2)}) collective-permute-start(f32[640,640]{1,0:T(8,128)S(1)} %collective-permute-done.42), channel_id=1, source_target_pairs={{0,3},{1,0},{2,1},{3,2},{4,7},{5,4},{6,5},{7,6},{8,11},{9,8},{10,9... | collective-permute-start | bytes 4915208 | tf_op jit(solution)/shard_map/ppermute | solution.py:21
  1006.2 38.6 %collective-permute-start.47 = (f32[640,640]{1,0:T(8,128)S(1)}, f32[640,640]{1,0:T(8,128)S(1)}, u32[]{:S(2)}, u32[]{:S(2)}) collective-permute-start(f32[640,640]{1,0:T(8,128)S(1)} %collective-permute-done.45), channel_id=1, source_target_pairs={{0,12},{4,0},{8,4},{12,8},{1,13},{5,1},{9,5},{13,9},{2,14},{6,2},{... | collective-permute-start | bytes 4915208 | tf_op jit(solution)/shard_map/ppermute | solution.py:22
  1013.7 34.3 %collective-permute-start.46 = (f32[640,640]{1,0:T(8,128)S(1)}, f32[640,640]{1,0:T(8,128)S(1)}, u32[]{:S(2)}, u32[]{:S(2)}) collective-permute-start(f32[640,640]{1,0:T(8,128)S(1)} %collective-permute-done.44), channel_id=1, source_target_pairs={{0,3},{1,0},{2,1},{3,2},{4,7},{5,4},{6,5},{7,6},{8,11},{9,8},{10,9... | collective-permute-start | bytes 4915208 | tf_op jit(solution)/shard_map/ppermute | solution.py:21
  (3 other events, 207.2 us)
where the time goes:
time: 1110 us
  starting transfers between devices  728 us (66%)
  waiting for transfers between devices  145 us (13%)
  matrix products  133 us (12%)
  blocking collectives  89.8 us (8%)
    ppermute x18, starting transfers between devices, grid_square(): left_block = lax.ppermute(left_block, 'col', shift_perm)  439 us
    ppermute x18, starting transfers between devices, grid_square(): right_block = lax.ppermute(right_block, 'row', shift_perm)  280 us
    dot_general x24, matrix products, block_product(): jnp.dot(left_block, right_block, preferred_element_type=jnp.float32, prec...  133 us
    ppermute x18, waiting for transfers between devices, grid_square(): right_block = lax.ppermute(right_block, 'row', shift_perm)  76.6 us
    ppermute x18, waiting for transfers between devices, grid_square(): left_block = lax.ppermute(left_block, 'col', shift_perm)  68.5 us
    psum x1, blocking collectives, local_run(): occ_list.append(lax.psum(jnp.sum(density * density), ('row', 'col')))  54.3 us
    psum x1, blocking collectives, local_run(): lax.psum(jnp.where(on_diag, jnp.trace(ham_block), 0.0), ('row', 'col'))  35.5 us
  transfers between devices with their start and end apart: 48, of which 21 were waited for; matrix products, arithmetic and copies ran while one was open for 9% of the time, Pallas kernels for 0%

commit v1 on v0

v1 whole, which is shorter than its diff:
```python
import functools

import jax
import jax.numpy as jnp
from jax import lax
from jax.experimental import pallas as pl
from jax.experimental.pallas import tpu as pltpu
from jax.sharding import PartitionSpec as P

F32 = jnp.float32
BF16 = jnp.bfloat16
MESH = pl.DeviceIdType.MESH
TERMS = ((0, 2), (2, 0), (1, 1), (0, 1), (1, 0), (0, 0))
NN = (((1,), (0,)), ((), ()))
NT = (((1,), (1,)), ((), ()))


def slab_of(label):
    return label // 2 + 2 * (1 - label % 2)


def kernel(steps, h_ref, bounds_ref, count_ref, flag_ref, out_ref, occ_ref, energy_ref,
           X, D, S, stats, part0, part1, g_send, g_recv, send, recv_x, recv_d, credit, p_send, p_recv):
    blk = h_ref.shape[0]
    T = 2 * blk // 5
    HB = 2 * blk
    order = 4 * blk
    sid, z, col = lax.axis_index("spin"), lax.axis_index("row"), lax.axis_index("col")
    y, c = col // 2, col % 2
    half = z // 2
    u = (y + half) % 2
    inner = (z + 1) // 2 % 2
    inner = jnp.int32(inner)
    sib_col, yp_col, sib_yp_col = 2 * y + 1 - c, 2 * (1 - y) + c, 2 * (1 - y) + 1 - c
    zp = z + 1 - 2 * (z % 2)
    opp = 3 - z
    outer = 3 * (z // 2)
    inner_z = 1 + half
    me = z * 4 + col

    def dev(zz, cc):
        return (sid, zz, cc)

    sib, ypart, zpart = dev(z, sib_col), dev(z, yp_col), dev(zp, col)

    def copy(src, dst, s_sem, r_sem, device):
        return pltpu.make_async_remote_copy(src_ref=src, dst_ref=dst, send_sem=s_sem, recv_sem=r_sem,
                                            device_id=device, device_id_type=MESH)

    def wait_recv(dst, r_sem):
        copy(dst, dst, g_send.at[0], r_sem, sib).wait_recv()

    def wait_send(src, s_sem):
        copy(src, src, s_sem, g_recv.at[0], sib).wait_send()

    def ds(index, size, step=None):
        return pl.ds(pl.multiple_of(index * (step or size), step or size), size)

    def block_at(zz, cc):
        row = (zz % 2) * blk
        column = ((cc // 2 + zz // 2) % 2) * HB + (cc % 2) * blk
        return X.at[0, pl.ds(pl.multiple_of(row, blk), blk), pl.ds(pl.multiple_of(column, blk), blk)]

    own_rows = ds(z % 2, blk)
    own_cols = ds(2 * u + c, blk)

    barrier = pltpu.get_barrier_semaphore()
    for dz in range(4):
        for dc in range(4):
            if dz or dc:
                pl.semaphore_signal(barrier, inc=1, device_id=dev((z + dz) % 4, (col + dc) % 4), device_id_type=MESH)
    pl.semaphore_wait(barrier, 15)

    def share(part):
        index = 0
        for dz in range(4):
            for dc in range(4):
                if dz or dc:
                    copy(part.at[me], part.at[me], p_send.at[index], p_recv.at[0],
                         dev((z + dz) % 4, (col + dc) % 4)).start()
                    index += 1

    def collect(part):
        wait_recv(part.at[pl.ds(0, 15)], p_recv.at[0])
        for index in range(15):
            wait_send(part.at[me], p_send.at[index])
        return jnp.sum(part[...], axis=0)

    copy(h_ref, block_at(z, col), g_send.at[1], g_recv.at[1], ypart).start()
    copy(h_ref, block_at(z, col), g_send.at[2], g_recv.at[2], zpart).start()
    copy(h_ref, block_at(z, col), g_send.at[0], g_recv.at[0], sib).start()
    X[0, own_rows, own_cols] = h_ref[...]
    row_id = lax.broadcasted_iota(jnp.int32, (blk, blk), 0) + z * blk
    col_id = lax.broadcasted_iota(jnp.int32, (blk, blk), 1) + col * blk
    part0[me] = jnp.full((8, 128), jnp.sum(jnp.where(row_id == col_id, h_ref[...], 0.0)), F32)
    share(part0)

    d_pieces = []
    for which in range(2):
        d_pieces.append((which, 0, 1))
        d_pieces.append((which, T, 2))

    def d_rows(which, zz):
        r = (zz + which) % 2
        return pl.ds(pl.multiple_of(r * blk, blk), blk)

    def d_send(which):
        @pl.when(jnp.logical_and(c == 0, inner == 1))
        def _():
            ud = 1 - u
            rows = d_rows(which, z)
            copy(X.at[0, rows, pl.ds(2 * T, T)], D.at[0, rows, pl.ds(0, T)],
                 g_send.at[7 + 2 * which], g_recv.at[7 + 2 * which], dev(opp, sib_col)).start()
            copy(X.at[0, rows, pl.ds(pl.multiple_of(ud * 3 * T, T), 2 * T)], D.at[0, rows, pl.ds(T, 2 * T)],
                 g_send.at[8 + 2 * which], g_recv.at[8 + 2 * which], dev(opp, sib_col)).start()

    wait_recv(block_at(z, yp_col), g_recv.at[1])
    copy(block_at(z, yp_col), block_at(z, yp_col), g_send.at[3], g_recv.at[3], sib).start()
    wait_recv(block_at(z, sib_col), g_recv.at[0])
    wait_recv(block_at(zp, col), g_recv.at[2])
    copy(block_at(zp, col), block_at(zp, col), g_send.at[5], g_recv.at[5], ypart).start()
    copy(block_at(zp, col), block_at(zp, col), g_send.at[4], g_recv.at[4], sib).start()
    wait_recv(block_at(z, sib_yp_col), g_recv.at[3])
    d_send(0)
    wait_recv(block_at(zp, yp_col), g_recv.at[5])
    copy(block_at(zp, yp_col), block_at(zp, yp_col), g_send.at[6], g_recv.at[6], sib).start()
    wait_recv(block_at(zp, sib_col), g_recv.at[4])
    wait_recv(block_at(zp, sib_yp_col), g_recv.at[6])
    d_send(1)
    src_z = 3 - inner_z

    def d_piece(which, first, count):
        return D.at[0, d_rows(which, src_z), pl.ds(first, count * T)]

    @pl.when(c == 1)
    def _():
        for index, (which, first, count) in enumerate(d_pieces):
            wait_recv(d_piece(which, first, count), g_recv.at[7 + index])

            @pl.when(inner == 1)
            def _():
                copy(d_piece(which, first, count), d_piece(which, first, count), g_send.at[7 + index],
                     g_recv.at[7 + index], dev(outer, col)).start()

    total = collect(part0)
    mu = total / order
    occupied = jnp.full((8, 128), count_ref[0], jnp.int32).astype(F32)
    scale = jnp.minimum(occupied / (bounds_ref[1] - mu), (order - occupied) / (mu - bounds_ref[0])) / order
    shift = occupied / order
    mu, scale, shift = mu[0:1, 0:1], scale[0:1, 0:1], shift[0:1, 0:1]

    for index in range(7):
        wait_send(h_ref, g_send.at[index])

    @pl.when(inner == 1)
    def _():
        for index, (which, first, count) in enumerate(d_pieces):
            wait_send(d_piece(which, first, count), g_send.at[7 + index])

    iota_r = lax.broadcasted_iota(jnp.int32, (T, T), 0)
    iota_c = lax.broadcasted_iota(jnp.int32, (T, T), 1)

    def start_tile(tile, slab_r, slab_c):
        diag = iota_r + slab_r * T == iota_c + slab_c * T
        return scale * (jnp.where(diag, mu, 0.0) - tile) + jnp.where(diag, shift, 0.0)

    def start_x(index, carry):
        i, k = index // 10, index % 10
        X[0, ds(i, T), ds(k, T)] = start_tile(X[0, ds(i, T), ds(k, T)], i, k)
        return carry

    lax.fori_loop(0, 50, start_x, 0)

    def set_slab(jj):
        return (2, 3 * u, 3 * u + 1)[jj]

    @pl.when(c == 1)
    def _():
        for jj in range(3):
            def start_d(k, carry):
                D[0, ds(k, T), ds(jj, T)] = start_tile(D[0, ds(k, T), ds(jj, T)], k, set_slab(jj))
                return carry

            lax.fori_loop(0, 5, start_d, 0)

    def split(index, tile):
        first = tile.astype(BF16)
        rest = tile - first.astype(F32)
        second = rest.astype(BF16)
        S[index, 0] = first
        S[index, 1] = second
        S[index, 2] = (rest - second.astype(F32)).astype(BF16)

    def product(left, right, dims):
        acc = None
        for a, b in TERMS:
            for k in range(10):
                term = lax.dot_general(S[left + k, a], S[right + k, b], dims, preferred_element_type=F32)
                acc = term if acc is None else acc + term
        return acc

    def member(label, who):
        return jnp.logical_or(label == 0, label % 2 == 1 - who)

    def x_tile(par, r, k):
        return X.at[par, ds(r, T), ds(k, T)]

    def d_tile(par, r, jj):
        return D.at[par, ds(r, T), ds(jj, T)]

    def d_place(i, s, who):
        in_s = member(s, who)
        return jnp.where(in_s, slab_of(i), slab_of(s)), jnp.where(in_s, (s + 1) // 2, (i + 1) // 2)

    def send0_drain(t):
        par = t % 2

        def stage(s, carry):
            def one(i, carry):
                n = s * (s + 1) // 2 + i
                wait_send(x_tile(0, 0, 0), send.at[par, n])

                @pl.when(i < s)
                def _():
                    wait_send(x_tile(0, 0, 0), send.at[par, 15 + n])

                needed = jnp.logical_or(member(s, 1 - u), member(i, 1 - u))

                @pl.when(jnp.logical_and(jnp.logical_and(inner == 1, t < steps), needed))
                def _():
                    wait_send(x_tile(0, 0, 0), send.at[par, 30 + n])
                return carry
            return lax.fori_loop(0, s + 1, one, carry)

        lax.fori_loop(0, 5, stage, 0)

    def send1_drain(t):
        par = t % 2

        def row(r, carry):
            for jj in range(3):
                wait_send(x_tile(0, 0, 0), send.at[par, 3 * r + jj])
                if jj:
                    wait_send(x_tile(0, 0, 0), send.at[par, 15 + 3 * r + jj])
            for q in range(2):
                wait_send(x_tile(0, 0, 0), send.at[par, 30 + 2 * r + q])

            @pl.when(jnp.logical_and(inner == 1, t < steps))
            def _():
                def one(i, carry):
                    @pl.when(jnp.logical_or(member(r, u), member(i, u)))
                    def _():
                        row_slab, jj = d_place(i, r, u)
                        wait_send(x_tile(0, 0, 0), send.at[par, 40 + 3 * row_slab + jj])
                    return carry
                lax.fori_loop(0, r + 1, one, 0)
            return carry

        lax.fori_loop(0, 5, row, 0)

    def step(t, carry):
        cur, nxt = t % 2, (t + 1) % 2
        flag = flag_ref[t].astype(F32)
        on_square, on_old = 2.0 * flag - 1.0, 2.0 - 2.0 * flag

        @pl.when(c == 0)
        def _():
            @pl.when(t >= 1)
            def _():
                pl.semaphore_wait(credit.at[0], 1)

                @pl.when(jnp.logical_and(inner == 1, t < steps - 1))
                def _():
                    pl.semaphore_wait(credit.at[2], 1)

            def stage(s, carry):
                gs = slab_of(s)

                @pl.when(t >= 1)
                def _():
                    for k in range(5, 10):
                        wait_recv(x_tile(cur, gs, k), recv_x.at[cur, gs * 10 + k])

                def split_one(k, carry):
                    split(s * 10 + k, X[cur, ds(gs, T), ds(k, T)])
                    return carry

                lax.fori_loop(0, 10, split_one, 0)

                def one(i, carry):
                    n = s * (s + 1) // 2 + i
                    gi = slab_of(i)
                    new = on_square * product(i * 10, s * 10, NT) + on_old * X[cur, ds(gi, T), ds(gs, T)]
                    X[nxt, ds(gi, T), ds(gs, T)] = new
                    copy(x_tile(nxt, gi, gs), x_tile(nxt, gi, gs), send.at[nxt, n], recv_x.at[nxt, gi * 10 + gs],
                         sib).start()

                    @pl.when(i < s)
                    def _():
                        X[nxt, ds(gs, T), ds(gi, T)] = X[nxt, ds(gi, T), ds(gs, T)].T
                        copy(x_tile(nxt, gs, gi), x_tile(nxt, gs, gi), send.at[nxt, 15 + n],
                             recv_x.at[nxt, gs * 10 + gi], sib).start()

                    who = 1 - u
                    across = jnp.logical_and(inner == 1, t < steps - 1)

                    @pl.when(jnp.logical_and(across, jnp.logical_or(member(s, who), member(i, who))))
                    def _():
                        row_slab, jj = d_place(i, s, who)
                        in_s = member(s, who)
                        src_r, src_c = jnp.where(in_s, gi, gs), jnp.where(in_s, gs, gi)
                        copy(x_tile(nxt, src_r, src_c), d_tile(nxt, row_slab, jj), send.at[nxt, 30 + n],
                             recv_d.at[nxt, 3 * row_slab + jj], dev(opp, sib_col)).start()
                    return carry

                return lax.fori_loop(0, s + 1, one, carry)

            lax.fori_loop(0, 5, stage, 0)

            @pl.when(t >= 1)
            def _():
                send0_drain(t)

        @pl.when(c == 1)
        def _():
            @pl.when(t >= 1)
            def _():
                pl.semaphore_wait(credit.at[0], 1)
                pl.semaphore_wait(credit.at[1], 1)

                @pl.when(jnp.logical_and(inner == 1, t < steps - 1))
                def _():
                    pl.semaphore_wait(credit.at[2], 1)

                for a, b in ((1, 0), (2, 0), (2, 1)):
                    D[cur, ds(set_slab(a), T), ds(b, T)] = D[cur, ds(set_slab(b), T), ds(a, T)].T

            for jj in range(3):
                def split_o(k, carry):
                    split(jj * 10 + k, X[cur, ds(k, T), ds(5 + set_slab(jj), T)])
                    split(jj * 10 + 5 + k, D[cur, ds(k, T), ds(jj, T)])
                    return carry

                lax.fori_loop(0, 5, split_o, 0)

            def forward(r):
                gr = slab_of(r)
                for q in range(2):
                    k = 5 + 3 * (1 - u) + q
                    wait_recv(x_tile(nxt, gr, k), recv_x.at[nxt, gr * 10 + k])
                    copy(x_tile(nxt, gr, k), x_tile(nxt, gr, k), send.at[nxt, 30 + 2 * r + q],
                         recv_x.at[nxt, gr * 10 + k], sib).start()

                @pl.when(t < steps - 1)
                def _():
                    def one(i, carry):
                        @pl.when(jnp.logical_or(member(r, u), member(i, u)))
                        def _():
                            row_slab, jj = d_place(i, r, u)
                            tile = d_tile(nxt, row_slab, jj)
                            wait_recv(tile, recv_d.at[nxt, 3 * row_slab + jj])

                            @pl.when(inner == 1)
                            def _():
                                copy(tile, tile, send.at[nxt, 40 + 3 * row_slab + jj],
                                     recv_d.at[nxt, 3 * row_slab + jj], dev(outer, col)).start()
                        return carry
                    lax.fori_loop(0, r + 1, one, 0)

            def row(r, carry):
                gr = slab_of(r)

                @pl.when(t >= 1)
                def _():
                    for k in range(5):
                        wait_recv(x_tile(cur, gr, k), recv_x.at[cur, gr * 10 + k])

                def split_one(k, carry):
                    split(30 + k, X[cur, ds(gr, T), ds(k, T)])
                    return carry

                lax.fori_loop(0, 10, split_one, 0)

                def one(jj, carry):
                    k = 5 + 2 * ((2 - jj) // 2) + ((jj + 1) // 2) * (3 * u + jj - 1)
                    new = on_square * product(30, jj * 10, NN) + on_old * X[cur, ds(gr, T), ds(k, T)]
                    X[nxt, ds(gr, T), ds(k, T)] = new
                    copy(x_tile(nxt, gr, k), x_tile(nxt, gr, k), send.at[nxt, 3 * r + jj],
                         recv_x.at[nxt, gr * 10 + k], sib).start()

                    @pl.when(jj > 0)
                    def _():
                        copy(x_tile(nxt, gr, k), x_tile(nxt, gr, k), send.at[nxt, 15 + 3 * r + jj],
                             recv_x.at[nxt, gr * 10 + k], ypart).start()
                    return carry

                lax.fori_loop(0, 3, one, 0)

                @pl.when(r >= 1)
                def _():
                    forward(r - 1)
                return carry

            lax.fori_loop(0, 5, row, 0)
            forward(4)

            @pl.when(t >= 1)
            def _():
                send1_drain(t)

        own = X[cur, own_rows, own_cols]
        line = lax.broadcasted_iota(jnp.int32, (8, 128), 0)
        stats[...] = jnp.where(line == t, jnp.sum(own * own), stats[...])

        @pl.when(t < steps - 1)
        def _():
            pl.semaphore_signal(credit.at[0], inc=1, device_id=sib, device_id_type=MESH)

            @pl.when(c == 1)
            def _():
                pl.semaphore_signal(credit.at[1], inc=1, device_id=ypart, device_id_type=MESH)

                @pl.when(t < steps - 2)
                def _():
                    @pl.when(inner == 1)
                    def _():
                        pl.semaphore_signal(credit.at[2], inc=1, device_id=dev(opp, sib_col), device_id_type=MESH)

                    @pl.when(inner == 0)
                    def _():
                        pl.semaphore_signal(credit.at[2], inc=1, device_id=dev(inner_z, col), device_id_type=MESH)
        return carry

    stats[...] = jnp.zeros_like(stats)
    lax.fori_loop(0, steps, step, 0)
    last = steps % 2

    def last_wait(r, carry):
        for k in range(5):
            where = 5 * (1 - c) + k
            wait_recv(x_tile(last, r, where), recv_x.at[last, r * 10 + where])
        return carry

    lax.fori_loop(0, 5, last_wait, 0)

    final = X[last, own_rows, own_cols]
    out_ref[...] = final
    line = lax.broadcasted_iota(jnp.int32, (8, 128), 0)
    part1[me] = jnp.where(line == steps, jnp.sum(final * h_ref[...]), stats[...])
    share(part1)

    @pl.when(c == 0)
    def _():
        send0_drain(steps)

    @pl.when(c == 1)
    def _():
        send1_drain(steps)

    total = collect(part1)
    for t in range(steps):
        occ_ref[t] = total[t, 0]
    energy_ref[0] = 2.0 * total[steps, 0]


def solution(mesh):
    def local_run(ham_block, bounds, occ_count, branches):
        blk = ham_block.shape[0]
        steps = branches.shape[0]
        T = 2 * blk // 5
        vmem, smem = pl.BlockSpec(memory_space=pltpu.VMEM), pl.BlockSpec(memory_space=pltpu.SMEM)
        return pl.pallas_call(
            functools.partial(kernel, steps),
            out_shape=(jax.ShapeDtypeStruct((blk, blk), F32), jax.ShapeDtypeStruct((steps,), F32),
                       jax.ShapeDtypeStruct((1,), F32)),
            in_specs=[vmem, smem, smem, smem],
            out_specs=(vmem, smem, smem),
            scratch_shapes=[
                pltpu.VMEM((2, 2 * blk, 4 * blk), F32),
                pltpu.VMEM((2, 2 * blk, 3 * T), F32),
                pltpu.VMEM((50, 3, T, T), BF16),
                pltpu.VMEM((8, 128), F32),
                pltpu.VMEM((16, 8, 128), F32),
                pltpu.VMEM((16, 8, 128), F32),
                pltpu.SemaphoreType.DMA((11,)),
                pltpu.SemaphoreType.DMA((11,)),
                pltpu.SemaphoreType.DMA((2, 55)),
                pltpu.SemaphoreType.DMA((2, 50)),
                pltpu.SemaphoreType.DMA((2, 15)),
                pltpu.SemaphoreType.REGULAR((3,)),
                pltpu.SemaphoreType.DMA((15,)),
                pltpu.SemaphoreType.DMA((1,)),
            ],
            compiler_params=pltpu.CompilerParams(collective_id=0, has_side_effects=True, vmem_limit_bytes=67043328),
        )(ham_block, bounds, occ_count, branches)

    return jax.shard_map(local_run, mesh=mesh, in_specs=(P(("spin", "row"), "col"), P("spin"), P("spin"), P("spin")), out_specs=(P(("spin", "row"), "col"), P("spin"), P("spin")), check_vma=False)
```

time: 1110 us -> 511 us (0.46)
  starting transfers between devices: 728 us -> 0 us
  Pallas kernels: 0 us -> 504 us
  waiting for transfers between devices: 145 us -> 0 us
  matrix products: 133 us -> 0 us
  blocking collectives: 89.8 us -> 0 us
    ppermute x48 -> x0, starting transfers between devices: 728 us -> none  [the longest x18 439 us: grid_square(): left_block = lax.ppermute(left_block, 'col', shift_perm)]
    pallas_call x0 -> x1, Pallas kernels: none -> 504 us  [local_run(): pl.pallas_call(functools.partial(kernel, steps), out_shape=(jax.ShapeDtyp...]
    ppermute x48 -> x0, waiting for transfers between devices: 145 us -> none  [the longest x18 76.6 us: grid_square(): right_block = lax.ppermute(right_block, 'row', shift_perm)]
    dot_general x24 -> x0, matrix products: 133 us -> none  [block_product(): jnp.dot(left_block, right_block, preferred_element_type=jnp.float32, prec...]
    psum x2 -> x0, blocking collectives: 89.8 us -> none  [the longest x1 54.3 us: local_run(): occ_list.append(lax.psum(jnp.sum(density * density), ('row', 'col')))]
  transfers between devices with their start and end apart: 48 -> 0, of which waited for: 21 -> 0; matrix products, arithmetic and copies ran while one was open for 9% -> 0% of each run, Pallas kernels for 0% -> 0%
where the time goes in v1:
time: 511 us; the launch traced here: 510 us
  Pallas kernels  504 us (99%)
    pallas_call x1, Pallas kernels, local_run(): pl.pallas_call(functools.partial(kernel, steps), out_shape=(jax.ShapeDtyp...  504 us

profile of v1, /device:TPU:0, one launch (start us, length us, event | category | flops | bytes accessed | tf_op | source)
XLA Modules:
  0.0 510.5 jit_solution(4813040509853240189)
XLA Ops:
  1.3 504.2 %shard_map.67 = (f32[640,640]{1,0:T(8,128)}, f32[6]{0:T(128)}, f32[1]{0:T(128)}) custom-call(f32[640,640]{1,0:T(8,128)} %h_ref.1, f32[2]{0:T(128)} %bounds_ref.1, s32[1]{0:T(128)S(6)} %copy.10.count_ref, s32[6]{0:T(128)} %flag_ref.1), custom_call_target="tpu_custom_call" | custom-call | tf_op jit(solution)/shard_map/pallas_call | solution.py:472
  505.5 0.0 copy-start
  505.5 2.7 copy.11
  508.2 0.0 copy-done
  508.2 0.5 copy.12
Async XLA Ops:
  505.5 2.7 copy-start

commit v2 on v1

--- a/solution.py
+++ b/solution.py
@@ -23,7 +23,6 @@
            X, D, S, stats, part0, part1, g_send, g_recv, send, recv_x, recv_d, credit, p_send, p_recv):
     blk = h_ref.shape[0]
     T = 2 * blk // 5
-    HB = 2 * blk
     order = 4 * blk
     sid, z, col = lax.axis_index("spin"), lax.axis_index("row"), lax.axis_index("col")
     y, c = col // 2, col % 2
@@ -53,16 +52,29 @@
     def wait_send(src, s_sem):
         copy(src, src, s_sem, g_recv.at[0], sib).wait_send()
 
-    def ds(index, size, step=None):
-        return pl.ds(pl.multiple_of(index * (step or size), step or size), size)
-
-    def block_at(zz, cc):
-        row = (zz % 2) * blk
-        column = ((cc // 2 + zz // 2) % 2) * HB + (cc % 2) * blk
-        return X.at[0, pl.ds(pl.multiple_of(row, blk), blk), pl.ds(pl.multiple_of(column, blk), blk)]
-
-    own_rows = ds(z % 2, blk)
-    own_cols = ds(2 * u + c, blk)
+    Q = T // 2
+
+    def spans(p):
+        return ((3 * p, 0, p * Q, T), (3 * p + 1, 0, p * Q + T, T), (2, p * Q, (1 - p) * 2 * T, Q))
+
+    def at(offset, size):
+        return pl.ds(offset if isinstance(offset, int) else pl.multiple_of(offset, Q), size)
+
+    def pieces(zz, cc):
+        first = 5 * ((cc // 2 + zz // 2) % 2)
+        out = []
+        for row, r_in, r_at, r_size in spans(zz % 2):
+            for column, c_in, c_at, c_size in spans(cc % 2):
+                out.append(((row, first + column, at(r_in, r_size), at(c_in, c_size)),
+                            (at(r_at, r_size), at(c_at, c_size))))
+        return out
+
+    own = pieces(z, col)
+
+    def send_block(zz, cc, s_sem, r_sem, device, fresh=False):
+        for there, here in pieces(zz, cc):
+            dst = X.at[(0, *there)]
+            copy(h_ref.at[here] if fresh else dst, dst, s_sem, r_sem, device).start()
 
     barrier = pltpu.get_barrier_semaphore()
     for dz in range(4):
@@ -86,61 +98,62 @@
             wait_send(part.at[me], p_send.at[index])
         return jnp.sum(part[...], axis=0)
 
-    copy(h_ref, block_at(z, col), g_send.at[1], g_recv.at[1], ypart).start()
-    copy(h_ref, block_at(z, col), g_send.at[2], g_recv.at[2], zpart).start()
-    copy(h_ref, block_at(z, col), g_send.at[0], g_recv.at[0], sib).start()
-    X[0, own_rows, own_cols] = h_ref[...]
+    send_block(z, col, g_send.at[1], g_recv.at[1], ypart, True)
+    send_block(z, col, g_send.at[2], g_recv.at[2], zpart, True)
+    send_block(z, col, g_send.at[0], g_recv.at[0], sib, True)
+    for there, here in own:
+        X[(0, *there)] = h_ref[here]
     row_id = lax.broadcasted_iota(jnp.int32, (blk, blk), 0) + z * blk
     col_id = lax.broadcasted_iota(jnp.int32, (blk, blk), 1) + col * blk
     part0[me] = jnp.full((8, 128), jnp.sum(jnp.where(row_id == col_id, h_ref[...], 0.0)), F32)
     share(part0)
 
-    d_pieces = []
-    for which in range(2):
-        d_pieces.append((which, 0, 1))
-        d_pieces.append((which, T, 2))
-
-    def d_rows(which, zz):
-        r = (zz + which) % 2
-        return pl.ds(pl.multiple_of(r * blk, blk), blk)
-
-    def d_send(which):
-        @pl.when(jnp.logical_and(c == 0, inner == 1))
+    def wait_block(r_sem):
+        wait_recv(out_ref, r_sem)
+
+    def d_slab(index, zz):
+        p = zz % 2
+        return (3 * p, 3 * p + 1, 2, 3 * (1 - p), 3 * (1 - p) + 1)[index]
+
+    def set_slab_of(jj, who):
+        return (2, 3 * who, 3 * who + 1)[jj]
+
+    def d_send(rows, when):
+        @pl.when(jnp.logical_and(jnp.logical_and(c == 0, inner == 1), when))
         def _():
-            ud = 1 - u
-            rows = d_rows(which, z)
-            copy(X.at[0, rows, pl.ds(2 * T, T)], D.at[0, rows, pl.ds(0, T)],
-                 g_send.at[7 + 2 * which], g_recv.at[7 + 2 * which], dev(opp, sib_col)).start()
-            copy(X.at[0, rows, pl.ds(pl.multiple_of(ud * 3 * T, T), 2 * T)], D.at[0, rows, pl.ds(T, 2 * T)],
-                 g_send.at[8 + 2 * which], g_recv.at[8 + 2 * which], dev(opp, sib_col)).start()
-
-    wait_recv(block_at(z, yp_col), g_recv.at[1])
-    copy(block_at(z, yp_col), block_at(z, yp_col), g_send.at[3], g_recv.at[3], sib).start()
-    wait_recv(block_at(z, sib_col), g_recv.at[0])
-    wait_recv(block_at(zp, col), g_recv.at[2])
-    copy(block_at(zp, col), block_at(zp, col), g_send.at[5], g_recv.at[5], ypart).start()
-    copy(block_at(zp, col), block_at(zp, col), g_send.at[4], g_recv.at[4], sib).start()
-    wait_recv(block_at(z, sib_yp_col), g_recv.at[3])
-    d_send(0)
-    wait_recv(block_at(zp, yp_col), g_recv.at[5])
-    copy(block_at(zp, yp_col), block_at(zp, yp_col), g_send.at[6], g_recv.at[6], sib).start()
-    wait_recv(block_at(zp, sib_col), g_recv.at[4])
-    wait_recv(block_at(zp, sib_yp_col), g_recv.at[6])
-    d_send(1)
-    src_z = 3 - inner_z
-
-    def d_piece(which, first, count):
-        return D.at[0, d_rows(which, src_z), pl.ds(first, count * T)]
+            for index in rows:
+                row = d_slab(index, z)
+                for jj in range(3):
+                    copy(X.at[0, row, set_slab_of(jj, 1 - u)], D.at[0, row, jj], send.at[0, 3 * index + jj],
+                         recv_d.at[0, 3 * index + jj], dev(opp, sib_col)).start()
+
+    wait_block(g_recv.at[0])
+    d_send((0, 1), u == 0)
+    wait_block(g_recv.at[1])
+    send_block(z, yp_col, g_send.at[3], g_recv.at[3], sib)
+    wait_block(g_recv.at[2])
+    send_block(zp, col, g_send.at[5], g_recv.at[5], ypart)
+    send_block(zp, col, g_send.at[4], g_recv.at[4], sib)
+    wait_block(g_recv.at[3])
+    d_send((0, 1), u == 1)
+    wait_block(g_recv.at[4])
+    d_send((2, 3, 4), u == 0)
+    wait_block(g_recv.at[5])
+    send_block(zp, yp_col, g_send.at[6], g_recv.at[6], sib)
+    wait_block(g_recv.at[6])
+    d_send((2, 3, 4), u == 1)
 
     @pl.when(c == 1)
     def _():
-        for index, (which, first, count) in enumerate(d_pieces):
-            wait_recv(d_piece(which, first, count), g_recv.at[7 + index])
-
-            @pl.when(inner == 1)
-            def _():
-                copy(d_piece(which, first, count), d_piece(which, first, count), g_send.at[7 + index],
-                     g_recv.at[7 + index], dev(outer, col)).start()
+        for index in range(5):
+            row = d_slab(index, 3 - inner_z)
+            for jj in range(3):
+                tile = D.at[0, row, jj]
+                wait_recv(tile, recv_d.at[0, 3 * index + jj])
+
+                @pl.when(inner == 1)
+                def _():
+                    copy(tile, tile, send.at[0, 3 * index + jj], recv_d.at[0, 3 * index + jj], dev(outer, col)).start()
 
     total = collect(part0)
     mu = total / order
@@ -150,12 +163,12 @@
     mu, scale, shift = mu[0:1, 0:1], scale[0:1, 0:1], shift[0:1, 0:1]
 
     for index in range(7):
-        wait_send(h_ref, g_send.at[index])
+        wait_send(out_ref, g_send.at[index])
 
     @pl.when(inner == 1)
     def _():
-        for index, (which, first, count) in enumerate(d_pieces):
-            wait_send(d_piece(which, first, count), g_send.at[7 + index])
+        for index in range(15):
+            wait_send(D.at[0, 0, 0], send.at[0, index])
 
     iota_r = lax.broadcasted_iota(jnp.int32, (T, T), 0)
     iota_c = lax.broadcasted_iota(jnp.int32, (T, T), 1)
@@ -166,19 +179,19 @@
 
     def start_x(index, carry):
         i, k = index // 10, index % 10
-        X[0, ds(i, T), ds(k, T)] = start_tile(X[0, ds(i, T), ds(k, T)], i, k)
+        X[0, i, k] = start_tile(X[0, i, k], i, k)
         return carry
 
     lax.fori_loop(0, 50, start_x, 0)
 
     def set_slab(jj):
-        return (2, 3 * u, 3 * u + 1)[jj]
+        return set_slab_of(jj, u)
 
     @pl.when(c == 1)
     def _():
         for jj in range(3):
             def start_d(k, carry):
-                D[0, ds(k, T), ds(jj, T)] = start_tile(D[0, ds(k, T), ds(jj, T)], k, set_slab(jj))
+                D[0, k, jj] = start_tile(D[0, k, jj], k, set_slab(jj))
                 return carry
 
             lax.fori_loop(0, 5, start_d, 0)
@@ -203,10 +216,10 @@
         return jnp.logical_or(label == 0, label % 2 == 1 - who)
 
     def x_tile(par, r, k):
-        return X.at[par, ds(r, T), ds(k, T)]
+        return X.at[par, r, k]
 
     def d_tile(par, r, jj):
-        return D.at[par, ds(r, T), ds(jj, T)]
+        return D.at[par, r, jj]
 
     def d_place(i, s, who):
         in_s = member(s, who)
@@ -258,6 +271,29 @@
 
         lax.fori_loop(0, 5, row, 0)
 
+    def forward_x(par, r):
+        gr = slab_of(r)
+        for q in range(2):
+            k = 5 + 3 * (1 - u) + q
+            wait_recv(x_tile(par, gr, k), recv_x.at[par, gr * 10 + k])
+            copy(x_tile(par, gr, k), x_tile(par, gr, k), send.at[par, 30 + 2 * r + q],
+                 recv_x.at[par, gr * 10 + k], sib).start()
+
+    def forward_d(par, s):
+        def one(i, carry):
+            @pl.when(jnp.logical_or(member(s, u), member(i, u)))
+            def _():
+                row_slab, jj = d_place(i, s, u)
+                tile = d_tile(par, row_slab, jj)
+                wait_recv(tile, recv_d.at[par, 3 * row_slab + jj])
+
+                @pl.when(inner == 1)
+                def _():
+                    copy(tile, tile, send.at[par, 40 + 3 * row_slab + jj],
+                         recv_d.at[par, 3 * row_slab + jj], dev(outer, col)).start()
+            return carry
+        lax.fori_loop(0, s + 1, one, 0)
+
     def step(t, carry):
         cur, nxt = t % 2, (t + 1) % 2
         flag = flag_ref[t].astype(F32)
@@ -265,14 +301,6 @@
 
         @pl.when(c == 0)
         def _():
-            @pl.when(t >= 1)
-            def _():
-                pl.semaphore_wait(credit.at[0], 1)
-
-                @pl.when(jnp.logical_and(inner == 1, t < steps - 1))
-                def _():
-                    pl.semaphore_wait(credit.at[2], 1)
-
             def stage(s, carry):
                 gs = slab_of(s)
 
@@ -282,7 +310,7 @@
                         wait_recv(x_tile(cur, gs, k), recv_x.at[cur, gs * 10 + k])
 
                 def split_one(k, carry):
-                    split(s * 10 + k, X[cur, ds(gs, T), ds(k, T)])
+                    split(s * 10 + k, X[cur, gs, k])
                     return carry
 
                 lax.fori_loop(0, 10, split_one, 0)
@@ -290,14 +318,23 @@
                 def one(i, carry):
                     n = s * (s + 1) // 2 + i
                     gi = slab_of(i)
-                    new = on_square * product(i * 10, s * 10, NT) + on_old * X[cur, ds(gi, T), ds(gs, T)]
-                    X[nxt, ds(gi, T), ds(gs, T)] = new
+                    new = on_square * product(i * 10, s * 10, NT) + on_old * X[cur, gi, gs]
+                    X[nxt, gi, gs] = new
+
+                    @pl.when(jnp.logical_and(n == 0, t >= 1))
+                    def _():
+                        pl.semaphore_wait(credit.at[0], 1)
+
+                        @pl.when(jnp.logical_and(inner == 1, t < steps - 1))
+                        def _():
+                            pl.semaphore_wait(credit.at[2], 1)
+
                     copy(x_tile(nxt, gi, gs), x_tile(nxt, gi, gs), send.at[nxt, n], recv_x.at[nxt, gi * 10 + gs],
                          sib).start()
 
                     @pl.when(i < s)
                     def _():
-                        X[nxt, ds(gs, T), ds(gi, T)] = X[nxt, ds(gi, T), ds(gs, T)].T
+                        X[nxt, gs, gi] = X[nxt, gi, gs].T
                         copy(x_tile(nxt, gs, gi), x_tile(nxt, gs, gi), send.at[nxt, 15 + n],
                              recv_x.at[nxt, gs * 10 + gi], sib).start()
 
@@ -323,49 +360,26 @@
 
         @pl.when(c == 1)
         def _():
+            for jj in range(3):
+                def split_o(k, carry):
+                    split(jj * 10 + k, X[cur, k, 5 + set_slab(jj)])
+                    return carry
+
+                lax.fori_loop(0, 5, split_o, 0)
+
             @pl.when(t >= 1)
             def _():
-                pl.semaphore_wait(credit.at[0], 1)
-                pl.semaphore_wait(credit.at[1], 1)
-
-                @pl.when(jnp.logical_and(inner == 1, t < steps - 1))
-                def _():
-                    pl.semaphore_wait(credit.at[2], 1)
-
+                forward_x(cur, 4)
+                forward_d(cur, 4)
                 for a, b in ((1, 0), (2, 0), (2, 1)):
-                    D[cur, ds(set_slab(a), T), ds(b, T)] = D[cur, ds(set_slab(b), T), ds(a, T)].T
+                    D[cur, set_slab(a), b] = D[cur, set_slab(b), a].T
 
             for jj in range(3):
-                def split_o(k, carry):
-                    split(jj * 10 + k, X[cur, ds(k, T), ds(5 + set_slab(jj), T)])
-                    split(jj * 10 + 5 + k, D[cur, ds(k, T), ds(jj, T)])
-                    return carry
-
-                lax.fori_loop(0, 5, split_o, 0)
-
-            def forward(r):
-                gr = slab_of(r)
-                for q in range(2):
-                    k = 5 + 3 * (1 - u) + q
-                    wait_recv(x_tile(nxt, gr, k), recv_x.at[nxt, gr * 10 + k])
-                    copy(x_tile(nxt, gr, k), x_tile(nxt, gr, k), send.at[nxt, 30 + 2 * r + q],
-                         recv_x.at[nxt, gr * 10 + k], sib).start()
-
-                @pl.when(t < steps - 1)
-                def _():
-                    def one(i, carry):
-                        @pl.when(jnp.logical_or(member(r, u), member(i, u)))
-                        def _():
-                            row_slab, jj = d_place(i, r, u)
-                            tile = d_tile(nxt, row_slab, jj)
-                            wait_recv(tile, recv_d.at[nxt, 3 * row_slab + jj])
-
-                            @pl.when(inner == 1)
-                            def _():
-                                copy(tile, tile, send.at[nxt, 40 + 3 * row_slab + jj],
-                                     recv_d.at[nxt, 3 * row_slab + jj], dev(outer, col)).start()
-                        return carry
-                    lax.fori_loop(0, r + 1, one, 0)
+                def split_p(k, carry):
+                    split(jj * 10 + 5 + k, D[cur, k, jj])
+                    return carry
+
+                lax.fori_loop(0, 5, split_p, 0)
 
             def row(r, carry):
                 gr = slab_of(r)
@@ -376,15 +390,25 @@
                         wait_recv(x_tile(cur, gr, k), recv_x.at[cur, gr * 10 + k])
 
                 def split_one(k, carry):
-                    split(30 + k, X[cur, ds(gr, T), ds(k, T)])
+                    split(30 + k, X[cur, gr, k])
                     return carry
 
                 lax.fori_loop(0, 10, split_one, 0)
 
                 def one(jj, carry):
                     k = 5 + 2 * ((2 - jj) // 2) + ((jj + 1) // 2) * (3 * u + jj - 1)
-                    new = on_square * product(30, jj * 10, NN) + on_old * X[cur, ds(gr, T), ds(k, T)]
-                    X[nxt, ds(gr, T), ds(k, T)] = new
+                    new = on_square * product(30, jj * 10, NN) + on_old * X[cur, gr, k]
+                    X[nxt, gr, k] = new
+
+                    @pl.when(jnp.logical_and(jnp.logical_and(r == 0, jj == 0), t >= 1))
+                    def _():
+                        pl.semaphore_wait(credit.at[0], 1)
+                        pl.semaphore_wait(credit.at[1], 1)
+
+                        @pl.when(jnp.logical_and(inner == 1, t < steps - 1))
+                        def _():
+                            pl.semaphore_wait(credit.at[2], 1)
+
                     copy(x_tile(nxt, gr, k), x_tile(nxt, gr, k), send.at[nxt, 3 * r + jj],
                          recv_x.at[nxt, gr * 10 + k], sib).start()
 
@@ -398,19 +422,22 @@
 
                 @pl.when(r >= 1)
                 def _():
-                    forward(r - 1)
+                    forward_x(nxt, r - 1)
+
+                    @pl.when(t < steps - 1)
+                    def _():
+                        forward_d(nxt, r - 1)
                 return carry
 
             lax.fori_loop(0, 5, row, 0)
-            forward(4)
 
             @pl.when(t >= 1)
             def _():
                 send1_drain(t)
 
-        own = X[cur, own_rows, own_cols]
         line = lax.broadcasted_iota(jnp.int32, (8, 128), 0)
-        stats[...] = jnp.where(line == t, jnp.sum(own * own), stats[...])
+        squares = sum(jnp.sum(jnp.square(X[(cur, *there)])) for there, _ in own)
+        stats[...] = jnp.where(line == t, squares, stats[...])
 
         @pl.when(t < steps - 1)
         def _():
@@ -434,6 +461,10 @@
     stats[...] = jnp.zeros_like(stats)
     lax.fori_loop(0, steps, step, 0)
     last = steps % 2
+
+    @pl.when(c == 1)
+    def _():
+        forward_x(last, 4)
 
     def last_wait(r, carry):
         for k in range(5):
@@ -443,10 +474,13 @@
 
     lax.fori_loop(0, 5, last_wait, 0)
 
-    final = X[last, own_rows, own_cols]
-    out_ref[...] = final
+    energy = jnp.float32(0.0)
+    for there, here in own:
+        final = X[(last, *there)]
+        out_ref[here] = final
+        energy += jnp.sum(final * h_ref[here])
     line = lax.broadcasted_iota(jnp.int32, (8, 128), 0)
-    part1[me] = jnp.where(line == steps, jnp.sum(final * h_ref[...]), stats[...])
+    part1[me] = jnp.where(line == steps, energy, stats[...])
     share(part1)
 
     @pl.when(c == 0)
@@ -476,8 +510,8 @@
             in_specs=[vmem, smem, smem, smem],
             out_specs=(vmem, smem, smem),
             scratch_shapes=[
-                pltpu.VMEM((2, 2 * blk, 4 * blk), F32),
-                pltpu.VMEM((2, 2 * blk, 3 * T), F32),
+                pltpu.VMEM((2, 5, 10, T, T), F32),
+                pltpu.VMEM((2, 5, 3, T, T), F32),
                 pltpu.VMEM((50, 3, T, T), BF16),
                 pltpu.VMEM((8, 128), F32),
                 pltpu.VMEM((16, 8, 128), F32),

time: 511 us -> 447 us (0.87)
  Pallas kernels: 504 us -> 441 us
    pallas_call x1, Pallas kernels: 504 us -> 441 us  [local_run(): pl.pallas_call(functools.partial(kernel, steps), out_shape=(jax.ShapeDtyp...]
where the time goes in v2:
time: 447 us
  Pallas kernels  441 us (99%)
    pallas_call x1, Pallas kernels, local_run(): pl.pallas_call(functools.partial(kernel, steps), out_shape=(jax.ShapeDtyp...  441 us

profile of v2, /device:TPU:0, one launch (start us, length us, event | category | flops | bytes accessed | tf_op | source)
XLA Modules:
  0.0 447.0 jit_solution(10120064672331535593)
XLA Ops:
  1.3 440.7 %shard_map.67 = (f32[640,640]{1,0:T(8,128)}, f32[6]{0:T(128)}, f32[1]{0:T(128)}) custom-call(f32[640,640]{1,0:T(8,128)} %h_ref.1, f32[2]{0:T(128)} %bounds_ref.1, s32[1]{0:T(128)S(6)} %copy.10.count_ref, s32[6]{0:T(128)} %flag_ref.1), custom_call_target="tpu_custom_call" | custom-call | tf_op jit(solution)/shard_map/pallas_call | solution.py:506
  442.0 0.0 copy-start
  442.0 2.7 copy.11
  444.7 0.0 copy-done
  444.7 0.5 copy.12
Async XLA Ops:
  442.0 2.7 copy-start

commit v3 on v2

--- a/solution.py
+++ b/solution.py
@@ -127,33 +127,48 @@
                     copy(X.at[0, row, set_slab_of(jj, 1 - u)], D.at[0, row, jj], send.at[0, 3 * index + jj],
                          recv_d.at[0, 3 * index + jj], dev(opp, sib_col)).start()
 
+    def relay(rows, when):
+        @pl.when(jnp.logical_and(c == 1, when))
+        def _():
+            for index in rows:
+                row = d_slab(index, 3 - inner_z)
+                for jj in range(3):
+                    tile = D.at[0, row, jj]
+                    wait_recv(tile, recv_d.at[0, 3 * index + jj])
+
+                    @pl.when(inner == 1)
+                    def _():
+                        copy(tile, tile, send.at[0, 3 * index + jj], recv_d.at[0, 3 * index + jj],
+                             dev(outer, col)).start()
+
+    over_y = jnp.logical_or(inner == 0, c == 0)
+    over_z = jnp.logical_and(inner == 0, c == 1)
     wait_block(g_recv.at[0])
     d_send((0, 1), u == 0)
     wait_block(g_recv.at[1])
+
+    @pl.when(over_z)
+    def _():
+        send_block(z, yp_col, g_send.at[7], g_recv.at[5], zpart)
+
     send_block(z, yp_col, g_send.at[3], g_recv.at[3], sib)
     wait_block(g_recv.at[2])
-    send_block(zp, col, g_send.at[5], g_recv.at[5], ypart)
+
+    @pl.when(over_y)
+    def _():
+        send_block(zp, col, g_send.at[5], g_recv.at[5], ypart)
+
     send_block(zp, col, g_send.at[4], g_recv.at[4], sib)
     wait_block(g_recv.at[3])
     d_send((0, 1), u == 1)
     wait_block(g_recv.at[4])
     d_send((2, 3, 4), u == 0)
+    early = jnp.logical_and(inner == 1, u == 1)
+    relay((0, 1), early)
     wait_block(g_recv.at[5])
     send_block(zp, yp_col, g_send.at[6], g_recv.at[6], sib)
     wait_block(g_recv.at[6])
     d_send((2, 3, 4), u == 1)
-
-    @pl.when(c == 1)
-    def _():
-        for index in range(5):
-            row = d_slab(index, 3 - inner_z)
-            for jj in range(3):
-                tile = D.at[0, row, jj]
-                wait_recv(tile, recv_d.at[0, 3 * index + jj])
-
-                @pl.when(inner == 1)
-                def _():
-                    copy(tile, tile, send.at[0, 3 * index + jj], recv_d.at[0, 3 * index + jj], dev(outer, col)).start()
 
     total = collect(part0)
     mu = total / order
@@ -162,14 +177,6 @@
     shift = occupied / order
     mu, scale, shift = mu[0:1, 0:1], scale[0:1, 0:1], shift[0:1, 0:1]
 
-    for index in range(7):
-        wait_send(out_ref, g_send.at[index])
-
-    @pl.when(inner == 1)
-    def _():
-        for index in range(15):
-            wait_send(D.at[0, 0, 0], send.at[0, index])
-
     iota_r = lax.broadcasted_iota(jnp.int32, (T, T), 0)
     iota_c = lax.broadcasted_iota(jnp.int32, (T, T), 1)
 
@@ -177,24 +184,29 @@
         diag = iota_r + slab_r * T == iota_c + slab_c * T
         return scale * (jnp.where(diag, mu, 0.0) - tile) + jnp.where(diag, shift, 0.0)
 
-    def start_x(index, carry):
-        i, k = index // 10, index % 10
-        X[0, i, k] = start_tile(X[0, i, k], i, k)
-        return carry
-
-    lax.fori_loop(0, 50, start_x, 0)
-
     def set_slab(jj):
         return set_slab_of(jj, u)
 
-    @pl.when(c == 1)
-    def _():
-        for jj in range(3):
-            def start_d(k, carry):
-                D[0, k, jj] = start_tile(D[0, k, jj], k, set_slab(jj))
-                return carry
-
-            lax.fori_loop(0, 5, start_d, 0)
+    relay((0, 1), jnp.logical_not(early))
+    relay((2, 3, 4), c == 1)
+
+    first_on = -scale
+    first_diag = scale * mu + shift
+
+    def old_tile(t, tile, slab_r, slab_c):
+        diag = iota_r + slab_r * T == iota_c + slab_c * T
+        first = (t == 0).astype(jnp.int32).astype(F32)
+        keep = 1.0 - first
+        return (first * first_on + keep) * tile + jnp.where(diag, first * first_diag, 0.0)
+
+    def split_first(t, index, tile, slab_r, slab_c):
+        @pl.when(t == 0)
+        def _():
+            split(index, start_tile(tile, slab_r, slab_c))
+
+        @pl.when(t > 0)
+        def _():
+            split(index, tile)
 
     def split(index, tile):
         first = tile.astype(BF16)
@@ -294,6 +306,27 @@
             return carry
         lax.fori_loop(0, s + 1, one, 0)
 
+    def send_tile(t, nxt, s, i):
+        n = s * (s + 1) // 2 + i
+        gs, gi = slab_of(s), slab_of(i)
+        s, i = jnp.int32(s), jnp.int32(i)
+        who = 1 - u
+        in_s = member(s, who)
+
+        @pl.when(jnp.logical_and(jnp.logical_and(inner == 1, t < steps - 1), jnp.logical_or(in_s, member(i, who))))
+        def _():
+            row_slab, jj = d_place(i, s, who)
+            src_r, src_c = jnp.where(in_s, gi, gs), jnp.where(in_s, gs, gi)
+            copy(x_tile(nxt, src_r, src_c), d_tile(nxt, row_slab, jj), send.at[nxt, 30 + n],
+                 recv_d.at[nxt, 3 * row_slab + jj], dev(opp, sib_col)).start()
+
+        copy(x_tile(nxt, gi, gs), x_tile(nxt, gi, gs), send.at[nxt, n], recv_x.at[nxt, gi * 10 + gs], sib).start()
+
+        @pl.when(i < s)
+        def _():
+            copy(x_tile(nxt, gs, gi), x_tile(nxt, gs, gi), send.at[nxt, 15 + n], recv_x.at[nxt, gs * 10 + gi],
+                 sib).start()
+
     def step(t, carry):
         cur, nxt = t % 2, (t + 1) % 2
         flag = flag_ref[t].astype(F32)
@@ -310,7 +343,7 @@
                         wait_recv(x_tile(cur, gs, k), recv_x.at[cur, gs * 10 + k])
 
                 def split_one(k, carry):
-                    split(s * 10 + k, X[cur, gs, k])
+                    split_first(t, s * 10 + k, X[cur, gs, k], gs, k)
                     return carry
 
                 lax.fori_loop(0, 10, split_one, 0)
@@ -318,10 +351,14 @@
                 def one(i, carry):
                     n = s * (s + 1) // 2 + i
                     gi = slab_of(i)
-                    new = on_square * product(i * 10, s * 10, NT) + on_old * X[cur, gi, gs]
+                    new = on_square * product(i * 10, s * 10, NT) + on_old * old_tile(t, X[cur, gi, gs], gi, gs)
                     X[nxt, gi, gs] = new
 
-                    @pl.when(jnp.logical_and(n == 0, t >= 1))
+                    @pl.when(i < s)
+                    def _():
+                        X[nxt, gs, gi] = X[nxt, gi, gs].T
+
+                    @pl.when(jnp.logical_and(n == 2, t >= 1))
                     def _():
                         pl.semaphore_wait(credit.at[0], 1)
 
@@ -329,25 +366,14 @@
                         def _():
                             pl.semaphore_wait(credit.at[2], 1)
 
-                    copy(x_tile(nxt, gi, gs), x_tile(nxt, gi, gs), send.at[nxt, n], recv_x.at[nxt, gi * 10 + gs],
-                         sib).start()
-
-                    @pl.when(i < s)
-                    def _():
-                        X[nxt, gs, gi] = X[nxt, gi, gs].T
-                        copy(x_tile(nxt, gs, gi), x_tile(nxt, gs, gi), send.at[nxt, 15 + n],
-                             recv_x.at[nxt, gs * 10 + gi], sib).start()
-
-                    who = 1 - u
-                    across = jnp.logical_and(inner == 1, t < steps - 1)
-
-                    @pl.when(jnp.logical_and(across, jnp.logical_or(member(s, who), member(i, who))))
-                    def _():
-                        row_slab, jj = d_place(i, s, who)
-                        in_s = member(s, who)
-                        src_r, src_c = jnp.where(in_s, gi, gs), jnp.where(in_s, gs, gi)
-                        copy(x_tile(nxt, src_r, src_c), d_tile(nxt, row_slab, jj), send.at[nxt, 30 + n],
-                             recv_d.at[nxt, 3 * row_slab + jj], dev(opp, sib_col)).start()
+                    @pl.when(n == 2)
+                    def _():
+                        send_tile(t, nxt, 0, 0)
+                        send_tile(t, nxt, 1, 0)
+
+                    @pl.when(n >= 2)
+                    def _():
+                        send_tile(t, nxt, s, i)
                     return carry
 
                 return lax.fori_loop(0, s + 1, one, carry)
@@ -362,7 +388,7 @@
         def _():
             for jj in range(3):
                 def split_o(k, carry):
-                    split(jj * 10 + k, X[cur, k, 5 + set_slab(jj)])
+                    split_first(t, jj * 10 + k, X[cur, k, 5 + set_slab(jj)], k, 5 + set_slab(jj))
                     return carry
 
                 lax.fori_loop(0, 5, split_o, 0)
@@ -376,7 +402,7 @@
 
             for jj in range(3):
                 def split_p(k, carry):
-                    split(jj * 10 + 5 + k, D[cur, k, jj])
+                    split_first(t, jj * 10 + 5 + k, D[cur, k, jj], k, set_slab(jj))
                     return carry
 
                 lax.fori_loop(0, 5, split_p, 0)
@@ -390,14 +416,14 @@
                         wait_recv(x_tile(cur, gr, k), recv_x.at[cur, gr * 10 + k])
 
                 def split_one(k, carry):
-                    split(30 + k, X[cur, gr, k])
+                    split_first(t, 30 + k, X[cur, gr, k], gr, k)
                     return carry
 
                 lax.fori_loop(0, 10, split_one, 0)
 
                 def one(jj, carry):
                     k = 5 + 2 * ((2 - jj) // 2) + ((jj + 1) // 2) * (3 * u + jj - 1)
-                    new = on_square * product(30, jj * 10, NN) + on_old * X[cur, gr, k]
+                    new = on_square * product(30, jj * 10, NN) + on_old * old_tile(t, X[cur, gr, k], gr, k)
                     X[nxt, gr, k] = new
 
                     @pl.when(jnp.logical_and(jnp.logical_and(r == 0, jj == 0), t >= 1))
@@ -437,7 +463,30 @@
 
         line = lax.broadcasted_iota(jnp.int32, (8, 128), 0)
         squares = sum(jnp.sum(jnp.square(X[(cur, *there)])) for there, _ in own)
-        stats[...] = jnp.where(line == t, squares, stats[...])
+
+        @pl.when(t > 0)
+        def _():
+            stats[...] = jnp.where(line == t, squares, stats[...])
+
+        @pl.when(t == 0)
+        def _():
+            start = scale * (jnp.where(row_id == col_id, mu, 0.0) - h_ref[...]) + jnp.where(row_id == col_id, shift, 0.0)
+            stats[...] = jnp.where(line == 0, jnp.sum(start * start), stats[...])
+            for index in (0, 1, 2, 3, 4, 6):
+                wait_send(out_ref, g_send.at[index])
+
+            @pl.when(over_y)
+            def _():
+                wait_send(out_ref, g_send.at[5])
+
+            @pl.when(over_z)
+            def _():
+                wait_send(out_ref, g_send.at[7])
+
+            @pl.when(inner == 1)
+            def _():
+                for index in range(15):
+                    wait_send(D.at[0, 0, 0], send.at[0, index])
 
         @pl.when(t < steps - 1)
         def _():

time: 447 us -> 428 us (0.957)
  Pallas kernels: 441 us -> 422 us
    pallas_call x1, Pallas kernels: 441 us -> 422 us  [local_run(): pl.pallas_call(functools.partial(kernel, steps), out_shape=(jax.ShapeDtyp...]
where the time goes in v3:
time: 428 us
  Pallas kernels  422 us (99%)
    pallas_call x1, Pallas kernels, local_run(): pl.pallas_call(functools.partial(kernel, steps), out_shape=(jax.ShapeDtyp...  422 us

profile of v3, /device:TPU:0, one launch (start us, length us, event | category | flops | bytes accessed | tf_op | source)
XLA Modules:
  0.0 427.8 jit_solution(4855534533997094320)
XLA Ops:
  1.3 421.6 %shard_map.67 = (f32[640,640]{1,0:T(8,128)}, f32[6]{0:T(128)}, f32[1]{0:T(128)}) custom-call(f32[640,640]{1,0:T(8,128)} %h_ref.1, f32[2]{0:T(128)} %bounds_ref.1, s32[1]{0:T(128)S(6)} %copy.10.count_ref, s32[6]{0:T(128)} %flag_ref.1), custom_call_target="tpu_custom_call" | custom-call | tf_op jit(solution)/shard_map/pallas_call | solution.py:555
  422.8 0.0 copy-start
  422.8 2.7 copy.11
  425.5 0.0 copy-done
  425.6 0.5 copy.12
Async XLA Ops:
  422.8 2.7 copy-start

commit v4 on v3

--- a/solution.py
+++ b/solution.py
@@ -20,7 +20,7 @@
 
 
 def kernel(steps, h_ref, bounds_ref, count_ref, flag_ref, out_ref, occ_ref, energy_ref,
-           X, D, S, stats, part0, part1, g_send, g_recv, send, recv_x, recv_d, credit, p_send, p_recv):
+           X, D, S, stats, part0, part1, g_send, g_recv, send, recv_x, recv_y, recv_d, credit, p_send, p_recv):
     blk = h_ref.shape[0]
     T = 2 * blk // 5
     order = 4 * blk
@@ -124,7 +124,7 @@
             for index in rows:
                 row = d_slab(index, z)
                 for jj in range(3):
-                    copy(X.at[0, row, set_slab_of(jj, 1 - u)], D.at[0, row, jj], send.at[0, 3 * index + jj],
+                    copy(X.at[0, row, set_slab_of(jj, 1 - u)], D.at[0, row, jj], g_send.at[8],
                          recv_d.at[0, 3 * index + jj], dev(opp, sib_col)).start()
 
     def relay(rows, when):
@@ -138,8 +138,7 @@
 
                     @pl.when(inner == 1)
                     def _():
-                        copy(tile, tile, send.at[0, 3 * index + jj], recv_d.at[0, 3 * index + jj],
-                             dev(outer, col)).start()
+                        copy(tile, tile, g_send.at[8], recv_d.at[0, 3 * index + jj], dev(outer, col)).start()
 
     over_y = jnp.logical_or(inner == 0, c == 0)
     over_z = jnp.logical_and(inner == 0, c == 1)
@@ -225,7 +224,7 @@
         return acc
 
     def member(label, who):
-        return jnp.logical_or(label == 0, label % 2 == 1 - who)
+        return jnp.logical_or(jnp.int32(label) == 0, label % 2 == 1 - who)
 
     def x_tile(par, r, k):
         return X.at[par, r, k]
@@ -237,59 +236,34 @@
         in_s = member(s, who)
         return jnp.where(in_s, slab_of(i), slab_of(s)), jnp.where(in_s, (s + 1) // 2, (i + 1) // 2)
 
-    def send0_drain(t):
-        par = t % 2
-
-        def stage(s, carry):
-            def one(i, carry):
-                n = s * (s + 1) // 2 + i
-                wait_send(x_tile(0, 0, 0), send.at[par, n])
-
-                @pl.when(i < s)
-                def _():
-                    wait_send(x_tile(0, 0, 0), send.at[par, 15 + n])
-
-                needed = jnp.logical_or(member(s, 1 - u), member(i, 1 - u))
-
-                @pl.when(jnp.logical_and(jnp.logical_and(inner == 1, t < steps), needed))
-                def _():
-                    wait_send(x_tile(0, 0, 0), send.at[par, 30 + n])
-                return carry
-            return lax.fori_loop(0, s + 1, one, carry)
-
-        lax.fori_loop(0, 5, stage, 0)
-
-    def send1_drain(t):
-        par = t % 2
-
-        def row(r, carry):
-            for jj in range(3):
-                wait_send(x_tile(0, 0, 0), send.at[par, 3 * r + jj])
-                if jj:
-                    wait_send(x_tile(0, 0, 0), send.at[par, 15 + 3 * r + jj])
-            for q in range(2):
-                wait_send(x_tile(0, 0, 0), send.at[par, 30 + 2 * r + q])
-
-            @pl.when(jnp.logical_and(inner == 1, t < steps))
-            def _():
-                def one(i, carry):
-                    @pl.when(jnp.logical_or(member(r, u), member(i, u)))
-                    def _():
-                        row_slab, jj = d_place(i, r, u)
-                        wait_send(x_tile(0, 0, 0), send.at[par, 40 + 3 * row_slab + jj])
-                    return carry
-                lax.fori_loop(0, r + 1, one, 0)
-            return carry
-
-        lax.fori_loop(0, 5, row, 0)
+    fifteen, twelve, ten, nine, six = (D.at[0], X.at[0, pl.ds(0, 4), pl.ds(0, 3)], X.at[0, 0],
+                                       X.at[0, pl.ds(0, 3), pl.ds(0, 3)], X.at[0, pl.ds(0, 2), pl.ds(0, 3)])
+    plane = z % 2
+
+    def send0_drain(par):
+        wait_send(fifteen, send.at[par, 0])
+        wait_send(ten, send.at[par, 1])
+
+        @pl.when(inner == 1)
+        def _():
+            wait_send(twelve, send.at[par, 2])
+
+    def send1_drain(par):
+        wait_send(fifteen, send.at[par, 0])
+        wait_send(ten, send.at[par, 1])
+        wait_send(ten, send.at[par, 3])
+
+        @pl.when(inner == 1)
+        def _():
+            wait_send(twelve, send.at[par, 2])
 
     def forward_x(par, r):
         gr = slab_of(r)
+        first = 5 + 3 * (1 - u)
+        wait_recv(X.at[par, gr, pl.ds(first, 2)], recv_y.at[par, gr])
         for q in range(2):
-            k = 5 + 3 * (1 - u) + q
-            wait_recv(x_tile(par, gr, k), recv_x.at[par, gr * 10 + k])
-            copy(x_tile(par, gr, k), x_tile(par, gr, k), send.at[par, 30 + 2 * r + q],
-                 recv_x.at[par, gr * 10 + k], sib).start()
+            tile = x_tile(par, gr, first + q)
+            copy(tile, tile, send.at[par, 3], recv_x.at[par, gr], sib).start()
 
     def forward_d(par, s):
         def one(i, carry):
@@ -301,13 +275,12 @@
 
                 @pl.when(inner == 1)
                 def _():
-                    copy(tile, tile, send.at[par, 40 + 3 * row_slab + jj],
+                    copy(tile, tile, send.at[par, 2],
                          recv_d.at[par, 3 * row_slab + jj], dev(outer, col)).start()
             return carry
         lax.fori_loop(0, s + 1, one, 0)
 
     def send_tile(t, nxt, s, i):
-        n = s * (s + 1) // 2 + i
         gs, gi = slab_of(s), slab_of(i)
         s, i = jnp.int32(s), jnp.int32(i)
         who = 1 - u
@@ -317,15 +290,14 @@
         def _():
             row_slab, jj = d_place(i, s, who)
             src_r, src_c = jnp.where(in_s, gi, gs), jnp.where(in_s, gs, gi)
-            copy(x_tile(nxt, src_r, src_c), d_tile(nxt, row_slab, jj), send.at[nxt, 30 + n],
+            copy(x_tile(nxt, src_r, src_c), d_tile(nxt, row_slab, jj), send.at[nxt, 2],
                  recv_d.at[nxt, 3 * row_slab + jj], dev(opp, sib_col)).start()
 
-        copy(x_tile(nxt, gi, gs), x_tile(nxt, gi, gs), send.at[nxt, n], recv_x.at[nxt, gi * 10 + gs], sib).start()
+        copy(x_tile(nxt, gi, gs), x_tile(nxt, gi, gs), send.at[nxt, 0], recv_x.at[nxt, gi], sib).start()
 
         @pl.when(i < s)
         def _():
-            copy(x_tile(nxt, gs, gi), x_tile(nxt, gs, gi), send.at[nxt, 15 + n], recv_x.at[nxt, gs * 10 + gi],
-                 sib).start()
+            copy(x_tile(nxt, gs, gi), x_tile(nxt, gs, gi), send.at[nxt, 1], recv_x.at[nxt, gs], sib).start()
 
     def step(t, carry):
         cur, nxt = t % 2, (t + 1) % 2
@@ -339,8 +311,7 @@
 
                 @pl.when(t >= 1)
                 def _():
-                    for k in range(5, 10):
-                        wait_recv(x_tile(cur, gs, k), recv_x.at[cur, gs * 10 + k])
+                    wait_recv(X.at[cur, gs, pl.ds(5, 5)], recv_x.at[cur, gs])
 
                 def split_one(k, carry):
                     split_first(t, s * 10 + k, X[cur, gs, k], gs, k)
@@ -349,7 +320,6 @@
                 lax.fori_loop(0, 10, split_one, 0)
 
                 def one(i, carry):
-                    n = s * (s + 1) // 2 + i
                     gi = slab_of(i)
                     new = on_square * product(i * 10, s * 10, NT) + on_old * old_tile(t, X[cur, gi, gs], gi, gs)
                     X[nxt, gi, gs] = new
@@ -358,31 +328,43 @@
                     def _():
                         X[nxt, gs, gi] = X[nxt, gi, gs].T
 
-                    @pl.when(jnp.logical_and(n == 2, t >= 1))
-                    def _():
-                        pl.semaphore_wait(credit.at[0], 1)
-
-                        @pl.when(jnp.logical_and(inner == 1, t < steps - 1))
+                    return carry
+
+                def needed(i, carry):
+                    full = t < steps - 1
+                    mine = jnp.logical_and(u == 0, jnp.logical_or(member(i, plane), member(s, plane)))
+
+                    @pl.when(jnp.logical_or(full, mine))
+                    def _():
+                        one(i, carry)
+
+                    @pl.when(s * (s + 1) // 2 + i == 2)
+                    def _():
+                        @pl.when(t >= 1)
                         def _():
-                            pl.semaphore_wait(credit.at[2], 1)
-
-                    @pl.when(n == 2)
-                    def _():
-                        send_tile(t, nxt, 0, 0)
-                        send_tile(t, nxt, 1, 0)
-
-                    @pl.when(n >= 2)
+                            pl.semaphore_wait(credit.at[0], 1)
+
+                            @pl.when(jnp.logical_and(inner == 1, full))
+                            def _():
+                                pl.semaphore_wait(credit.at[2], 1)
+
+                        @pl.when(jnp.logical_or(full, u == 0))
+                        def _():
+                            send_tile(t, nxt, 0, 0)
+                            send_tile(t, nxt, 1, 0)
+
+                    @pl.when(jnp.logical_and(s * (s + 1) // 2 + i >= 2, jnp.logical_or(full, mine)))
                     def _():
                         send_tile(t, nxt, s, i)
                     return carry
 
-                return lax.fori_loop(0, s + 1, one, carry)
+                return lax.fori_loop(0, s + 1, needed, carry)
 
             lax.fori_loop(0, 5, stage, 0)
 
             @pl.when(t >= 1)
             def _():
-                send0_drain(t)
+                send0_drain(cur)
 
         @pl.when(c == 1)
         def _():
@@ -412,8 +394,22 @@
 
                 @pl.when(t >= 1)
                 def _():
-                    for k in range(5):
-                        wait_recv(x_tile(cur, gr, k), recv_x.at[cur, gr * 10 + k])
+                    wait_recv(X.at[cur, gr, pl.ds(0, 5)], recv_x.at[cur, gr])
+
+                @pl.when(jnp.logical_or(t < steps - 1, member(r, plane)))
+                def _():
+                    active_row(r, gr)
+
+                @pl.when(jnp.logical_and(r >= 1, jnp.logical_or(t < steps - 1, member(r - 1, plane))))
+                def _():
+                    forward_x(nxt, r - 1)
+
+                    @pl.when(t < steps - 1)
+                    def _():
+                        forward_d(nxt, r - 1)
+                return carry
+
+            def active_row(r, gr):
 
                 def split_one(k, carry):
                     split_first(t, 30 + k, X[cur, gr, k], gr, k)
@@ -435,31 +431,20 @@
                         def _():
                             pl.semaphore_wait(credit.at[2], 1)
 
-                    copy(x_tile(nxt, gr, k), x_tile(nxt, gr, k), send.at[nxt, 3 * r + jj],
-                         recv_x.at[nxt, gr * 10 + k], sib).start()
+                    copy(x_tile(nxt, gr, k), x_tile(nxt, gr, k), send.at[nxt, 0], recv_x.at[nxt, gr], sib).start()
 
                     @pl.when(jj > 0)
                     def _():
-                        copy(x_tile(nxt, gr, k), x_tile(nxt, gr, k), send.at[nxt, 15 + 3 * r + jj],
-                             recv_x.at[nxt, gr * 10 + k], ypart).start()
+                        copy(x_tile(nxt, gr, k), x_tile(nxt, gr, k), send.at[nxt, 1], recv_y.at[nxt, gr], ypart).start()
                     return carry
 
                 lax.fori_loop(0, 3, one, 0)
 
-                @pl.when(r >= 1)
-                def _():
-                    forward_x(nxt, r - 1)
-
-                    @pl.when(t < steps - 1)
-                    def _():
-                        forward_d(nxt, r - 1)
-                return carry
-
             lax.fori_loop(0, 5, row, 0)
 
             @pl.when(t >= 1)
             def _():
-                send1_drain(t)
+                send1_drain(cur)
 
         line = lax.broadcasted_iota(jnp.int32, (8, 128), 0)
         squares = sum(jnp.sum(jnp.square(X[(cur, *there)])) for there, _ in own)
@@ -485,8 +470,7 @@
 
             @pl.when(inner == 1)
             def _():
-                for index in range(15):
-                    wait_send(D.at[0, 0, 0], send.at[0, index])
+                wait_send(D.at[0], g_send.at[8])
 
         @pl.when(t < steps - 1)
         def _():
@@ -511,17 +495,25 @@
     lax.fori_loop(0, steps, step, 0)
     last = steps % 2
 
-    @pl.when(c == 1)
+    @pl.when(jnp.logical_and(c == 1, member(4, plane)))
     def _():
         forward_x(last, 4)
 
-    def last_wait(r, carry):
-        for k in range(5):
-            where = 5 * (1 - c) + k
-            wait_recv(x_tile(last, r, where), recv_x.at[last, r * 10 + where])
-        return carry
-
-    lax.fori_loop(0, 5, last_wait, 0)
+    for r in range(5):
+        active = member(r, plane)
+        gr = slab_of(r)
+
+        @pl.when(jnp.logical_and(c == 0, active))
+        def _():
+            wait_recv(X.at[last, gr, pl.ds(5, 5)], recv_x.at[last, gr])
+
+        @pl.when(jnp.logical_and(jnp.logical_and(c == 1, u == 0), active))
+        def _():
+            wait_recv(X.at[last, gr, pl.ds(0, 5)], recv_x.at[last, gr])
+
+        @pl.when(jnp.logical_and(jnp.logical_and(c == 1, u == 0), jnp.logical_not(active)))
+        def _():
+            wait_recv(X.at[last, gr, pl.ds(0, 3)], recv_x.at[last, gr])
 
     energy = jnp.float32(0.0)
     for there, here in own:
@@ -532,13 +524,16 @@
     part1[me] = jnp.where(line == steps, energy, stats[...])
     share(part1)
 
-    @pl.when(c == 0)
+    @pl.when(jnp.logical_and(c == 0, u == 0))
     def _():
-        send0_drain(steps)
+        wait_send(twelve, send.at[last, 0])
+        wait_send(nine, send.at[last, 1])
 
     @pl.when(c == 1)
     def _():
-        send1_drain(steps)
+        wait_send(nine, send.at[last, 0])
+        wait_send(six, send.at[last, 1])
+        wait_send(six, send.at[last, 3])
 
     total = collect(part1)
     for t in range(steps):
@@ -567,8 +562,9 @@
                 pltpu.VMEM((16, 8, 128), F32),
                 pltpu.SemaphoreType.DMA((11,)),
                 pltpu.SemaphoreType.DMA((11,)),
-                pltpu.SemaphoreType.DMA((2, 55)),
-                pltpu.SemaphoreType.DMA((2, 50)),
+                pltpu.SemaphoreType.DMA((2, 4)),
+                pltpu.SemaphoreType.DMA((2, 5)),
+                pltpu.SemaphoreType.DMA((2, 5)),
                 pltpu.SemaphoreType.DMA((2, 15)),
                 pltpu.SemaphoreType.REGULAR((3,)),
                 pltpu.SemaphoreType.DMA((15,)),

time: 428 us -> 423 us (0.988)
  Pallas kernels: 422 us -> 417 us
    pallas_call x1, Pallas kernels: 422 us -> 417 us  [local_run(): pl.pallas_call(functools.partial(kernel, steps), out_shape=(jax.ShapeDtyp...]
where the time goes in v4:
time: 423 us
  Pallas kernels  417 us (99%)
    pallas_call x1, Pallas kernels, local_run(): pl.pallas_call(functools.partial(kernel, steps), out_shape=(jax.ShapeDtyp...  417 us

profile of v4, /device:TPU:0, one launch (start us, length us, event | category | flops | bytes accessed | tf_op | source)
XLA Modules:
  0.0 422.9 jit_solution(6019919470291150510)
XLA Ops:
  1.3 416.7 %shard_map.67 = (f32[640,640]{1,0:T(8,128)}, f32[6]{0:T(128)}, f32[1]{0:T(128)}) custom-call(f32[640,640]{1,0:T(8,128)} %h_ref.1, f32[2]{0:T(128)} %bounds_ref.1, s32[1]{0:T(128)S(6)} %copy.10.count_ref, s32[6]{0:T(128)} %flag_ref.1), custom_call_target="tpu_custom_call" | custom-call | tf_op jit(solution)/shard_map/pallas_call | solution.py:550
  417.9 0.0 copy-start
  417.9 2.7 copy.11
  420.6 0.0 copy-done
  420.7 0.5 copy.12
Async XLA Ops:
  417.9 2.7 copy-start

commit v5 on v4

--- a/solution.py
+++ b/solution.py
@@ -265,7 +265,7 @@
             tile = x_tile(par, gr, first + q)
             copy(tile, tile, send.at[par, 3], recv_x.at[par, gr], sib).start()
 
-    def forward_d(par, s):
+    def forward_d(par, s, low, high):
         def one(i, carry):
             @pl.when(jnp.logical_or(member(s, u), member(i, u)))
             def _():
@@ -278,7 +278,7 @@
                     copy(tile, tile, send.at[par, 2],
                          recv_d.at[par, 3 * row_slab + jj], dev(outer, col)).start()
             return carry
-        lax.fori_loop(0, s + 1, one, 0)
+        lax.fori_loop(low, high, one, 0)
 
     def send_tile(t, nxt, s, i):
         gs, gi = slab_of(s), slab_of(i)
@@ -378,7 +378,7 @@
             @pl.when(t >= 1)
             def _():
                 forward_x(cur, 4)
-                forward_d(cur, 4)
+                forward_d(cur, 4, 2, 5)
                 for a, b in ((1, 0), (2, 0), (2, 1)):
                     D[cur, set_slab(a), b] = D[cur, set_slab(b), a].T
 
@@ -400,13 +400,17 @@
                 def _():
                     active_row(r, gr)
 
+                @pl.when(jnp.logical_and(t < steps - 1, r < 4))
+                def _():
+                    @pl.when(jnp.logical_and(inner == 1, jnp.logical_and(r == 0, t >= 1)))
+                    def _():
+                        pl.semaphore_wait(credit.at[2], 1)
+
+                    forward_d(nxt, r, 0, r + 1)
+
                 @pl.when(jnp.logical_and(r >= 1, jnp.logical_or(t < steps - 1, member(r - 1, plane))))
                 def _():
                     forward_x(nxt, r - 1)
-
-                    @pl.when(t < steps - 1)
-                    def _():
-                        forward_d(nxt, r - 1)
                 return carry
 
             def active_row(r, gr):
@@ -427,15 +431,15 @@
                         pl.semaphore_wait(credit.at[0], 1)
                         pl.semaphore_wait(credit.at[1], 1)
 
-                        @pl.when(jnp.logical_and(inner == 1, t < steps - 1))
-                        def _():
-                            pl.semaphore_wait(credit.at[2], 1)
-
                     copy(x_tile(nxt, gr, k), x_tile(nxt, gr, k), send.at[nxt, 0], recv_x.at[nxt, gr], sib).start()
 
                     @pl.when(jj > 0)
                     def _():
                         copy(x_tile(nxt, gr, k), x_tile(nxt, gr, k), send.at[nxt, 1], recv_y.at[nxt, gr], ypart).start()
+
+                    @pl.when(jnp.logical_and(jnp.logical_and(r == 4, jj == 1), t < steps - 1))
+                    def _():
+                        forward_d(nxt, 4, 0, 2)
                     return carry
 
                 lax.fori_loop(0, 3, one, 0)

time: 423 us -> 404 us (0.955)
  Pallas kernels: 417 us -> 398 us
    pallas_call x1, Pallas kernels: 417 us -> 398 us  [local_run(): pl.pallas_call(functools.partial(kernel, steps), out_shape=(jax.ShapeDtyp...]
where the time goes in v5:
time: 404 us
  Pallas kernels  398 us (99%)
    pallas_call x1, Pallas kernels, local_run(): pl.pallas_call(functools.partial(kernel, steps), out_shape=(jax.ShapeDtyp...  398 us

profile of v5, /device:TPU:0, one launch (start us, length us, event | category | flops | bytes accessed | tf_op | source)
XLA Modules:
  0.0 404.0 jit_solution(14901137102899647655)
XLA Ops:
  1.3 397.7 %shard_map.67 = (f32[640,640]{1,0:T(8,128)}, f32[6]{0:T(128)}, f32[1]{0:T(128)}) custom-call(f32[640,640]{1,0:T(8,128)} %h_ref.1, f32[2]{0:T(128)} %bounds_ref.1, s32[1]{0:T(128)S(6)} %copy.10.count_ref, s32[6]{0:T(128)} %flag_ref.1), custom_call_target="tpu_custom_call" | custom-call | tf_op jit(solution)/shard_map/pallas_call | solution.py:554
  399.0 0.0 copy-start
  399.0 2.7 copy.11
  401.7 0.0 copy-done
  401.7 0.5 copy.12
Async XLA Ops:
  399.0 2.7 copy-start

commit v6 on v5

--- a/solution.py
+++ b/solution.py
@@ -378,7 +378,7 @@
             @pl.when(t >= 1)
             def _():
                 forward_x(cur, 4)
-                forward_d(cur, 4, 2, 5)
+                forward_d(cur, 4, 3, 5)
                 for a, b in ((1, 0), (2, 0), (2, 1)):
                     D[cur, set_slab(a), b] = D[cur, set_slab(b), a].T
 
@@ -399,14 +399,6 @@
                 @pl.when(jnp.logical_or(t < steps - 1, member(r, plane)))
                 def _():
                     active_row(r, gr)
-
-                @pl.when(jnp.logical_and(t < steps - 1, r < 4))
-                def _():
-                    @pl.when(jnp.logical_and(inner == 1, jnp.logical_and(r == 0, t >= 1)))
-                    def _():
-                        pl.semaphore_wait(credit.at[2], 1)
-
-                    forward_d(nxt, r, 0, r + 1)
 
                 @pl.when(jnp.logical_and(r >= 1, jnp.logical_or(t < steps - 1, member(r - 1, plane))))
                 def _():
@@ -437,9 +429,13 @@
                     def _():
                         copy(x_tile(nxt, gr, k), x_tile(nxt, gr, k), send.at[nxt, 1], recv_y.at[nxt, gr], ypart).start()
 
-                    @pl.when(jnp.logical_and(jnp.logical_and(r == 4, jj == 1), t < steps - 1))
-                    def _():
-                        forward_d(nxt, 4, 0, 2)
+                    @pl.when(jnp.logical_and(jj == 1, t < steps - 1))
+                    def _():
+                        @pl.when(jnp.logical_and(inner == 1, jnp.logical_and(r == 0, t >= 1)))
+                        def _():
+                            pl.semaphore_wait(credit.at[2], 1)
+
+                        forward_d(nxt, r, 0, r + 1 - 2 * (r // 4))
                     return carry
 
                 lax.fori_loop(0, 3, one, 0)

time: 404 us -> 412 us (1.020)
  Pallas kernels: 398 us -> 406 us
    pallas_call x1, Pallas kernels: 398 us -> 406 us  [local_run(): pl.pallas_call(functools.partial(kernel, steps), out_shape=(jax.ShapeDtyp...]
where the time goes in v6:
time: 412 us
  Pallas kernels  406 us (99%)
    pallas_call x1, Pallas kernels, local_run(): pl.pallas_call(functools.partial(kernel, steps), out_shape=(jax.ShapeDtyp...  406 us

profile of v6, /device:TPU:0, one launch (start us, length us, event | category | flops | bytes accessed | tf_op | source)
XLA Modules:
  0.0 412.3 jit_solution(16732225834560857646)
XLA Ops:
  1.3 406.0 %shard_map.67 = (f32[640,640]{1,0:T(8,128)}, f32[6]{0:T(128)}, f32[1]{0:T(128)}) custom-call(f32[640,640]{1,0:T(8,128)} %h_ref.1, f32[2]{0:T(128)} %bounds_ref.1, s32[1]{0:T(128)S(6)} %copy.10.count_ref, s32[6]{0:T(128)} %flag_ref.1), custom_call_target="tpu_custom_call" | custom-call | tf_op jit(solution)/shard_map/pallas_call | solution.py:550
  407.3 0.0 copy-start
  407.3 2.7 copy.11
  410.0 0.0 copy-done
  410.0 0.5 copy.12
Async XLA Ops:
  407.3 2.7 copy-start
